TPU v7x, 32 devices: a whole 2x2x4 slice. The times are simulated.
32 devices in a mesh: gx: 4 (over y, x), gy: 4 (over z), gz: 2 (over core).
Axes of the slice: x: 2, y: 2, z: 4, core: 2. Of those that a mesh axis runs over, the one named last changes fastest.
Arguments:
- rhs_coarse: bfloat16 [32, 32, 128], P('gx'), may hold values from -24 to 24
- rhs_mid: bfloat16 [64, 64, 256], P('gx', 'gy'), may hold values from -24 to 24
- rhs_fine: bfloat16 [128, 128, 512], P('gx', 'gy', 'gz'), may hold values from -24 to 24
- occupied_coarse: int32 [4, 4, 16], P('gx'), may hold values 0 or 1
- occupied_mid: int32 [8, 8, 32], P('gx', 'gy'), may hold values 0 or 1
- occupied_fine: int32 [16, 16, 64], P('gx', 'gy', 'gz'), may hold values 0 or 1
- screen_weight: float32 [3], replicated, may hold values from 0.2 to 2
Outputs:
- solution_coarse: float32 [32, 32, 128], P('gx')
- solution_mid: float32 [64, 64, 256], P('gx', 'gy')
- solution_fine: float32 [128, 128, 512], P('gx', 'gy', 'gz')
All inputs are finite; a program needn't handle non-finite values. No bound on the sum of `occupied_coarse` or of `occupied_mid` or of `occupied_fine` on one device may be relied on, other than what follows from the above.
Results may differ from a plain program's by a relative error of at most 0.0003.
Values sent between devices are 32-bit elements; how exact they have to be, the bound alone decides.
A program may use at most 128 MiB of HBM per device.

v0:
```python
import functools

import jax
import jax.numpy as jnp
from jax import lax
from jax.experimental import pallas as pl
from jax.experimental.pallas import tpu as pltpu
from jax.sharding import PartitionSpec as P

MESH = pl.DeviceIdType.MESH
F32 = jnp.float32
BF16 = jnp.bfloat16
PAD = 4
ROWS = 8
LANES = 128


def iota(shape, dim):
    return lax.broadcasted_iota(jnp.int32, shape, dim)


def logical(index, own, extra):
    if extra == 0:
        return index
    return jnp.where(index < own + extra // 2, index, index - (own + extra))


def prolong_matrix(fine, coarse, total, fine_dim):
    base = lax.shift_right_arithmetic(fine, 1)
    beside = base + 2 * (fine & 1) - 1
    inside = jnp.logical_and(fine >= 0, fine < total)
    value = jnp.where(coarse == base, 0.75, jnp.where(coarse == beside, 0.25, 0.0))
    return jnp.where(inside, value, 0.0).astype(BF16)


def split(values):
    high = values.astype(BF16)
    return high, (values - high.astype(F32)).astype(BF16)


def mm(a, b):
    return jnp.dot(a, b, preferred_element_type=F32)


def fold_rows(values):
    total = values[0:ROWS]
    for row in range(ROWS, values.shape[0], ROWS):
        total = total + values[row : row + ROWS]
    out = total[:, 0:LANES]
    for lane in range(LANES, values.shape[1], LANES):
        out = out + total[:, lane : lane + LANES]
    return out


def coefficients(m0, n1, n2, n3):
    rho = n1 / m0
    spread = n2 - rho * n1
    bent = 6.0 * spread + (n3 - 2.0 * rho * n2 + rho * rho * n1)
    turn = jnp.where(bent > 0.0, jnp.maximum(spread, 0.0) / bent, 0.0)
    first = m0 / ((6.0 + rho) * m0 - jnp.maximum(spread, 0.0) * turn)
    second = -first * turn
    return first - second * rho, second


def kernel(
    dims,
    rhs_c, rhs_m, rhs_f, occ_c, occ_m, occ_f, weight,
    out_c, out_m, out_f,
    cr, cw, cs, cx, ctz, ct, oc,
    mb, mg, mr, mw, ms, mx, mtz, mt, om, m_up, m_dn, m_fu, m_fd, om_l, om_r,
    fb, fg, fr, fw, fs, of, f_up, f_dn, f_fu, f_fd, of_l, of_r,
    ac, am, af, ag, ss, rs, sc, rc, sm, rm, sf, rf, sg, rg,
):
    nx, ny, nz = dims
    ix, iy, iz = lax.axis_index("gx"), lax.axis_index("gy"), lax.axis_index("gz")
    xc, yc, zc = rhs_c.shape
    xm, ym, zm = rhs_m.shape
    xf, yf, zf = rhs_f.shape
    bc, bm, bf = occ_c.shape, occ_m.shape, occ_f.shape
    x_low, x_high = ix > 0, ix < nx - 1
    y_low, y_high = iy > 0, iy < ny - 1

    for ref in (oc, om, of):
        ref[...] = jnp.zeros_like(ref)
    cr[PAD : PAD + xc] = rhs_c[...].astype(F32)
    oc[1 : 1 + bc[0], 0 : bc[1], 0 : bc[2]] = occ_c[...].astype(F32)
    om[1 : 1 + bm[0], 0 : bm[1], 0 : bm[2]] = occ_m[...].astype(F32)
    of[1 : 1 + bf[0], 0 : bf[1], 0 : bf[2]] = occ_f[...].astype(F32)
    mb[PAD : PAD + xm, 0:ym, :] = rhs_m[...].astype(F32)

    def fill_fine(x, carry):
        fb[x + PAD, 0:yf, 0:zf] = rhs_f[x].astype(F32)
        return carry

    lax.fori_loop(0, xf, fill_fine, 0)

    barrier = pltpu.get_barrier_semaphore()
    flat = [(a, b, 0) for a in range(nx) for b in range(ny)][1:]
    across = [(0, 0, c) for c in range(1, nz)]
    peers = flat + across

    def at(offset):
        return (
            lax.rem(ix + offset[0], nx), lax.rem(iy + offset[1], ny), lax.rem(iz + offset[2], nz)
        )

    for offset in peers:
        pl.semaphore_signal(barrier, inc=1, device_id=at(offset), device_id_type=MESH)

    @pl.when(jnp.logical_not(x_low))
    def _():
        cr[0:4] = jnp.zeros((4, yc, zc), F32)
        mb[1:4, 0:ym, :] = jnp.zeros((3, ym, zm), F32)
        fb[2:4, 0:yf, :] = jnp.zeros((2, yf, fb.shape[2]), F32)

    @pl.when(jnp.logical_not(x_high))
    def _():
        cr[PAD + xc : PAD + xc + 4] = jnp.zeros((4, yc, zc), F32)
        mb[PAD + xm : PAD + xm + 3, 0:ym, :] = jnp.zeros((3, ym, zm), F32)
        fb[PAD + xf : PAD + xf + 2, 0:yf, :] = jnp.zeros((2, yf, fb.shape[2]), F32)

    @pl.when(jnp.logical_not(x_low))
    def _():
        for ref, reach in ((m_fu, 3), (m_fd, 3), (f_fu, 2), (f_fd, 2)):
            ref[0:reach] = jnp.zeros((reach,) + tuple(ref.shape[1:]), F32)
        for ref in (om_l, om_r, of_l, of_r):
            ref[0:1] = jnp.zeros((1,) + tuple(ref.shape[1:]), F32)

    @pl.when(jnp.logical_not(x_high))
    def _():
        for ref, reach in ((m_fu, 3), (m_fd, 3), (f_fu, 2), (f_fd, 2)):
            size = ref.shape[0]
            ref[size - reach : size] = jnp.zeros((reach,) + tuple(ref.shape[1:]), F32)
        for ref in (om_l, om_r, of_l, of_r):
            size = ref.shape[0]
            ref[size - 1 : size] = jnp.zeros((1,) + tuple(ref.shape[1:]), F32)

    @pl.when(jnp.logical_not(y_low))
    def _():
        for ref in (m_fu, f_fu, om_l, of_l):
            ref[...] = jnp.zeros_like(ref)

    @pl.when(jnp.logical_not(y_high))
    def _():
        for ref in (m_fd, f_fd, om_r, of_r):
            ref[...] = jnp.zeros_like(ref)

    pl.semaphore_wait(barrier, len(peers))

    used = [0]

    def copy(src, dst, target):
        k = used[0]
        used[0] += 1
        return pltpu.make_async_remote_copy(
            src_ref=src, dst_ref=dst, send_sem=ss.at[k], recv_sem=rs.at[k],
            device_id=target, device_id_type=MESH,
        )

    def start(items):
        for c, can_send, _ in items:
            if can_send is None:
                c.start()
            else:
                pl.when(can_send)(c.start)

    def arrive(items):
        for c, _, can_recv in items:
            if can_recv is None:
                c.wait_recv()
            else:
                pl.when(can_recv)(c.wait_recv)

    def left(items):
        for c, can_send, _ in items:
            if can_send is None:
                c.wait_send()
            else:
                pl.when(can_send)(c.wait_send)

    def x_swap(ref, occ, own, rows, width, bricks):
        items = []
        up, down = {"gx": ix + 1}, {"gx": ix - 1}
        items.append((copy(ref.at[PAD + own - width : PAD + own, 0:rows, :],
                           ref.at[PAD - width : PAD, 0:rows, :], up), x_high, x_low))
        items.append((copy(ref.at[PAD : PAD + width, 0:rows, :],
                           ref.at[PAD + own : PAD + own + width, 0:rows, :], down), x_low, x_high))
        items.append((copy(occ.at[bricks], occ.at[0], up), x_high, x_low))
        items.append((copy(occ.at[1], occ.at[bricks + 1], down), x_low, x_high))
        return items

    x_coarse = x_swap(cr, oc, xc, yc, 4, bc[0])
    start(x_coarse)

    def y_swap(ref, occ, own, rows, width, reach, to_up, to_down, from_low, from_high, occ_l, occ_r, bricks):
        planes, flags = pl.ds(reach, own), pl.ds(1, bricks)
        to_up[planes] = ref[PAD : PAD + own, rows - width : rows, :]
        to_down[planes] = ref[PAD : PAD + own, 0:width, :]
        items = []
        for out, dst, occ_dst, step, can_send, can_recv in (
            (to_up, from_low, occ_l, 1, y_high, y_low), (to_down, from_high, occ_r, -1, y_low, y_high)
        ):
            side = {"gy": iy + step}
            items.append((copy(out.at[planes], dst.at[planes], side), can_send, can_recv))
            items.append((copy(occ.at[flags], occ_dst.at[flags], side), can_send, can_recv))
            corner = {"gx": ix + 1, "gy": iy + step}
            when = (jnp.logical_and(can_send, x_high), jnp.logical_and(can_recv, x_low))
            items.append((copy(out.at[pl.ds(own, reach)], dst.at[pl.ds(0, reach)], corner), *when))
            items.append((copy(occ.at[bricks], occ_dst.at[0], corner), *when))
            corner = {"gx": ix - 1, "gy": iy + step}
            when = (jnp.logical_and(can_send, x_low), jnp.logical_and(can_recv, x_high))
            items.append(
                (copy(out.at[pl.ds(reach, reach)], dst.at[pl.ds(own + reach, reach)], corner), *when)
            )
            items.append((copy(occ.at[1], occ_dst.at[bricks + 1], corner), *when))
        return items

    def y_merge(ref, own, width, from_low, from_high, planes):
        first, count = planes
        parts = [from_high[...], from_low[...]]
        if 2 * width < ROWS:
            parts.insert(1, jnp.zeros((count, ROWS - 2 * width, ref.shape[2]), F32))
        ref[first : first + count, own : own + ROWS, :] = jnp.concatenate(parts, axis=1)

    mid_planes, fine_planes = (1, xm + 6), (2, xf + 4)

    def row_prolong(own, extra, index, total, cols, col_own, col_extra, col_index):
        shape = (own + extra, cols)
        fine = logical(iota(shape, 0), own, extra) + own * index
        coarse = logical(iota(shape, 1), col_own, col_extra) + col_own * col_index
        return prolong_matrix(fine, coarse, total, 0)

    def lane_prolong(own, extra, index, total, rows):
        shape = (rows, own + extra)
        fine = logical(iota(shape, 1), own, extra) + own * index
        return prolong_matrix(fine, iota(shape, 0), total, 1)

    def screens(dest, occ_parts, own, extra_rows, bricks_y, lane_matrix, level):
        count = dest.shape[0]
        side = own // bricks_y
        cols = ROWS * len(occ_parts)
        shape = (dest.shape[1], cols)
        brick = lax.div(logical(iota(shape, 0), own, extra_rows) + side, side) - 1
        place = jnp.where(
            brick < 0, ROWS + bricks_y - 1, jnp.where(brick >= bricks_y, 2 * ROWS, brick)
        )
        row_matrix = (place == iota(shape, 1)).astype(BF16)
        for x in range(count):
            flags = jnp.concatenate([part[x] for part in occ_parts], axis=0).astype(BF16)
            wide = mm(flags, lane_matrix).astype(BF16)
            dest[x] = weight[level] * (0.25 + mm(row_matrix, wide))

    def along_y(v):
        n = v.shape[0]
        return pltpu.roll(v, 1, 0), pltpu.roll(v, n - 1, 0)

    def along_z(v):
        n = v.shape[1]
        return pltpu.roll(v, 1, 1), pltpu.roll(v, n - 1, 1)

    lanes_c = (iota((LANES, zc), 0) == lax.div(iota((LANES, zc), 1), zc // bc[2])).astype(BF16)
    arrive(x_coarse)
    halo_mid = x_swap(mb, om, xm, ym, 3, bm[0])
    halo_mid += y_swap(mb, om, xm, ym, 4, 3, m_up, m_dn, m_fu, m_fd, om_l, om_r, bm[0])
    start(halo_mid)
    z_fine = []
    if nz == 2:
        target = {"gz": 1 - iz}
        low = pl.ds(pl.multiple_of((1 - iz) * (zf - LANES), LANES), LANES)
        z_fine.append((copy(
            fb.at[PAD : PAD + xf, 0:yf, low],
            fb.at[PAD : PAD + xf, 0:yf, zf : zf + LANES], target), None, None))
        z_fine.append((copy(
            of.at[1 : 1 + bf[0], :, 0:LANES], of.at[1 : 1 + bf[0], :, LANES : 2 * LANES],
            target), None, None))
    else:
        fb[PAD : PAD + xf, 0:yf, zf:] = jnp.zeros((xf, yf, LANES), F32)
    start(z_fine)
    screens(cs, [oc], yc, 0, bc[1], lanes_c, 0)
    side_c = xc // bc[0]
    shape_c = (yc, zc)
    row_c, lane_c = iota(shape_c, 0), iota(shape_c, 1)

    def sum_c(v, both):
        yu, yd = along_y(v)
        zu, zd = along_z(v)
        total = jnp.where(row_c < yc - 1, yd, 0.0) + jnp.where(lane_c < zc - 1, zd, 0.0)
        if both:
            total = total + jnp.where(row_c > 0, yu, 0.0) + jnp.where(lane_c > 0, zu, 0.0)
        return total

    def coarse_w(p, carry):
        r = cr[p]
        place = xc * ix + p - PAD
        keep = jnp.logical_and(place >= 0, place < xc * nx).astype(F32)
        screen = cs[lax.div(p + (side_c - PAD), side_c)]
        cw[p] = keep * (screen * r - (cr[p - 1] + cr[p + 1] + sum_c(r, True)))
        return carry

    lax.fori_loop(1, xc + 7, coarse_w, 0, unroll=7)

    def coarse_moments(p, acc):
        r, w = cr[p], cw[p]
        screen = cs[lax.div(p + (side_c - PAD), side_c)]
        image = screen * w - 2.0 * (cw[p + 1] + sum_c(w, False))
        return tuple(a + fold_rows(b) for a, b in zip(acc, (r * r, r * w, w * w, w * image)))

    zero = jnp.zeros((ROWS, LANES), F32)

    def spread(value, buf, send, recv, offsets, slot):
        buf[slot] = value
        copies = []
        for k, offset in enumerate(offsets):
            c = pltpu.make_async_remote_copy(
                src_ref=buf.at[slot], dst_ref=buf.at[slot], send_sem=send.at[k],
                recv_sem=recv.at[k], device_id=at(offset), device_id_type=MESH,
            )
            c.start()
            copies.append(c)
        return copies

    def stacked(acc):
        parts = [jnp.sum(a, axis=0, keepdims=True) for a in acc]
        return jnp.concatenate(parts + [jnp.zeros((ROWS - 4, LANES), F32)], axis=0)

    def gathered(copies, buf):
        for c in copies:
            c.wait_recv()
        total = buf[0]
        for k in range(1, buf.shape[0]):
            total = total + buf[k]
        return total

    def solve(total):
        total = jnp.sum(total, axis=1, keepdims=True)
        return coefficients(*[total[k : k + 1] for k in range(4)])

    acc = lax.fori_loop(PAD, PAD + xc, coarse_moments, (zero,) * 4, unroll=4)
    coarse_copies = spread(
        stacked(acc), ac, sc, rc, [(d, 0, 0) for d in range(1, nx)], ix
    )

    arrive(z_fine)
    halo_fine = x_swap(fb, of, xf, yf, 2, bf[0])
    halo_fine += y_swap(fb, of, xf, yf, 2, 2, f_up, f_dn, f_fu, f_fd, of_l, of_r, bf[0])
    start(halo_fine)
    mid_lanes = lane_prolong(zm, 0, 0, zm, zc)
    mid_rows = row_prolong(ym, ROWS, iy, ym * ny, yc, yc, 0, 0)
    ka, kb = solve(gathered(coarse_copies, ac))
    for j in range(xc + 6):
        cx[j] = ka * cr[j + 1] + kb * cw[j + 1]
    out_c[...] = cx[3 : 3 + xc]

    def prolong(src, tz, dst, lane_matrix, row_matrix):
        n, rows, lanes = src.shape
        high, low = split(src[...].reshape(n * rows, lanes))
        tz[...] = (mm(high, lane_matrix) + mm(low, lane_matrix)).reshape(tz.shape)
        for j in range(n):
            high, low = split(tz[j])
            dst[j] = mm(row_matrix, high) + mm(row_matrix, low)

    def interpolate(t, g, own, first, total):
        for p in range(own + 2 * PAD):
            m = p - PAD
            j = m // 2
            beside = min(max(j + (1 if m % 2 else -1) - first, 0), t.shape[0] - 1)
            place = own * ix + m
            keep = jnp.logical_and(place >= 0, place < total).astype(F32)
            g[p] = (0.75 * keep) * t[j - first] + (0.25 * keep) * t[beside]

    def neighbours(v, low_lane, high_lane):
        yu, yd = along_y(v)
        zu, zd = along_z(v)
        if low_lane is not None:
            zu, zd = jnp.where(low_lane, 0.0, zu), jnp.where(high_lane, 0.0, zd)
        return yu + yd + zu + zd

    def later(v, high_lane):
        yd = along_y(v)[1]
        zd = along_z(v)[1]
        if high_lane is not None:
            zd = jnp.where(high_lane, 0.0, zd)
        return yd + zd

    def run_depth(b, g, r, w, s, own, rows, lanes, reach, side, ends, mask):
        low_lane, high_lane = ends
        total_x = own * nx

        def inside(p):
            place = own * ix + p - PAD
            return jnp.logical_and(place >= 0, place < total_x).astype(F32)

        def brick(p):
            return lax.div(p + (side - PAD), side)

        def make_r(p, carry):
            c = g[p]
            value = b[p] - (6.0 + s[brick(p)]) * c
            value = value + (g[p - 1] + g[p + 1]) + neighbours(c, low_lane, high_lane)
            r[p] = value * (mask * inside(p))
            return carry

        lax.fori_loop(PAD - reach, PAD + own + reach, make_r, 0, unroll=6)

        def make_w(p, carry):
            c = r[p]
            value = s[brick(p)] * c - (r[p - 1] + r[p + 1]) - neighbours(c, low_lane, high_lane)
            w[p] = value * (mask * inside(p))
            return carry

        lax.fori_loop(PAD - reach + 1, PAD + own + 1 + (reach - 2), make_w, 0, unroll=6)

        def moments(p, acc):
            rv, wv = r[p, 0:rows, 0:lanes], w[p, 0:rows, 0:lanes]
            full = w[p]
            image = s[brick(p), 0:rows, 0:lanes] * wv - 2.0 * (
                w[p + 1, 0:rows, 0:lanes] + later(full, high_lane)[0:rows, 0:lanes]
            )
            return tuple(
                a + fold_rows(v) for a, v in zip(acc, (rv * rv, rv * wv, wv * wv, wv * image))
            )

        return lax.fori_loop(PAD, PAD + own, moments, (zero,) * 4, unroll=8)

    prolong(cx, ctz, ct, mid_lanes, mid_rows)
    interpolate(ct, mg, xm, -3, xm * nx)
    arrive(halo_mid)
    left(halo_mid)
    y_merge(mb, ym, 4, m_fu, m_fd, mid_planes)
    lanes_m = (iota((LANES, zm), 0) == lax.div(iota((LANES, zm), 1), zm // bm[2])).astype(BF16)
    screens(ms, [om, om_l, om_r], ym, ROWS, bm[1], lanes_m, 1)
    shape_m = (ym + ROWS, zm)
    row_m = logical(iota(shape_m, 0), ym, ROWS) + ym * iy
    mask_m = jnp.logical_and(row_m >= 0, row_m < ym * ny).astype(F32)
    ends_m = (iota(shape_m, 1) == 0, iota(shape_m, 1) == zm - 1)
    acc = run_depth(mb, mg, mr, mw, ms, xm, ym, zm, 3, xm // bm[0], ends_m, mask_m)
    mid_copies = spread(stacked(acc), am, sm, rm, flat, ix * ny + iy)

    arrive(halo_fine)
    left(halo_fine)
    left(z_fine)
    y_merge(fb, yf, 2, f_fu, f_fd, fine_planes)
    shape_e = (2 * LANES, zf + LANES)
    cell = logical(iota(shape_e, 1), zf, LANES)
    side_z = zf // bf[2]
    brick = lax.div(cell + side_z * LANES, side_z) - LANES
    place = jnp.where(
        brick < 0, LANES + bf[2] + brick, jnp.where(brick >= bf[2], LANES + brick - bf[2], brick)
    )
    lanes_f = (place == iota(shape_e, 0)).astype(BF16)
    screens(fs, [of, of_l, of_r], yf, ROWS, bf[1], lanes_f, 2)
    shape_f = (yf + ROWS, zf + LANES)
    row_f = logical(iota(shape_f, 0), yf, ROWS) + yf * iy
    lane_f = logical(iota(shape_f, 1), zf, LANES) + zf * iz
    mask_f = jnp.logical_and(
        jnp.logical_and(row_f >= 0, row_f < yf * ny), jnp.logical_and(lane_f >= 0, lane_f < zf * nz)
    ).astype(F32)
    fine_lanes = lane_prolong(zf, LANES, iz, zf * nz, zm)
    fine_rows = row_prolong(yf, ROWS, iy, yf * ny, ym + ROWS, ym, ROWS, iy)
    ka, kb = solve(gathered(mid_copies, am))
    for p in range(2, xm + 6):
        value = mg[p] + ka * mr[p] + kb * mw[p]
        mx[p - 2] = value
        if PAD <= p < PAD + xm:
            out_m[p - PAD] = value[0:ym]

    prolong(mx, mtz, mt, fine_lanes, fine_rows)
    interpolate(mt, fg, xf, -2, xf * nx)
    acc = run_depth(fb, fg, fr, fw, fs, xf, yf, zf, 2, xf // bf[0], (None, None), mask_f)
    fine_copies = spread(stacked(acc), af, sf, rf, flat, ix * ny + iy)
    total = gathered(fine_copies, af)
    last_copies = spread(total, ag, sg, rg, across, iz)
    ka, kb = solve(gathered(last_copies, ag))

    def finish(x, carry):
        p = x + PAD
        out_f[x] = (
            fg[p, 0:yf, 0:zf] + ka * fr[p, 0:yf, 0:zf] + kb * fw[p, 0:yf, 0:zf]
        )
        return carry

    lax.fori_loop(0, xf, finish, 0, unroll=4)

    left(x_coarse)
    for c in coarse_copies + mid_copies + fine_copies + last_copies:
        c.wait_send()


def shards(dims, *args):
    nx, ny, nz = dims
    rhs_c, rhs_m, rhs_f, occ_c, occ_m, occ_f, _ = args
    xc, yc, zc = rhs_c.shape
    xm, ym, zm = rhs_m.shape
    xf, yf, zf = rhs_f.shape
    me, fe = (ym + ROWS, zm), (yf + ROWS, zf + LANES)

    def buf(*shape):
        return pltpu.VMEM(shape, F32)

    bm, bf = occ_m.shape[0] + 2, occ_f.shape[0] + 2
    scratch = [
        buf(xc + 8, yc, zc), buf(xc + 8, yc, zc), buf(occ_c.shape[0] + 2, yc, zc),
        buf(xc + 6, yc, zc), buf(xc + 6, yc, zm), buf(xc + 6, *me),
        buf(occ_c.shape[0] + 2, ROWS, LANES),
        buf(xm + 8, *me), buf(xm + 8, *me), buf(xm + 8, *me), buf(xm + 8, *me), buf(bm, *me),
        buf(xm + 4, *me), buf(xm + 4, me[0], fe[1]), buf(xm + 4, *fe),
        buf(bm, ROWS, LANES),
        buf(xm + 6, 4, zm), buf(xm + 6, 4, zm), buf(xm + 6, 4, zm), buf(xm + 6, 4, zm),
        buf(bm, ROWS, LANES), buf(bm, ROWS, LANES),
        buf(xf + 8, *fe), buf(xf + 8, *fe), buf(xf + 8, *fe), buf(xf + 8, *fe), buf(bf, *fe),
        buf(bf, ROWS, 2 * LANES),
        buf(xf + 4, 2, fe[1]), buf(xf + 4, 2, fe[1]), buf(xf + 4, 2, fe[1]), buf(xf + 4, 2, fe[1]),
        buf(bf, ROWS, 2 * LANES), buf(bf, ROWS, 2 * LANES),
        buf(nx, ROWS, LANES), buf(nx * ny, ROWS, LANES), buf(nx * ny, ROWS, LANES),
        buf(nz, ROWS, LANES),
    ]
    for count in (40, nx, nx * ny, nx * ny, nz):
        scratch += [pltpu.SemaphoreType.DMA((count,))] * 2
    vmem = pl.BlockSpec(memory_space=pltpu.VMEM)
    return pl.pallas_call(
        functools.partial(kernel, dims),
        out_shape=[pltpu.VMEM(a.shape, F32) for a in args[:3]],
        in_specs=[vmem] * 6 + [pl.BlockSpec(memory_space=pltpu.SMEM)],
        out_specs=[vmem] * 3,
        scratch_shapes=scratch,
        compiler_params=pltpu.CompilerParams(
            collective_id=0, has_side_effects=True, vmem_limit_bytes=60 * 1024 * 1024
        ),
    )(*args)


def solution(mesh):
    dims = tuple(mesh.shape[axis] for axis in ("gx", "gy", "gz"))
    in_specs = (
        P("gx", None, None), P("gx", "gy", None), P("gx", "gy", "gz"),
        P("gx", None, None), P("gx", "gy", None), P("gx", "gy", "gz"), P(),
    )
    out_specs = (P("gx", None, None), P("gx", "gy", None), P("gx", "gy", "gz"))
    return jax.shard_map(
        functools.partial(shards, dims), mesh=mesh, in_specs=in_specs, out_specs=out_specs,
        check_vma=False,
    )
```

profile of v0, /device:TPU:0, one launch (start us, length us, event | category | flops | bytes accessed | tf_op | source)
XLA Modules:
  0.0 40.7 jit_solution(8359447661493429291)
XLA Ops:
  0.6 37.8 %shard_map.94 = (f32[8,32,128]{2,1,0:T(8,128)S(1)}, f32[16,16,256]{2,1,0:T(8,128)S(1)}, f32[32,32,256]{2,1,0:T(8,128)S(1)}) custom-call(bf16[8,32,128]{2,1,0:T(8,128)(2,1)} %rhs_c.1, bf16[16,16,256]{2,1,0:T(8,128)(2,1)} %rhs_m.1, bf16[32,32,256]{2,1,0:T(8,128)(2,1)} %rhs_f.1, s32[1,4,16]{2,1,0:T(4,128)} %occ_c.1, s32[2,2,32]{2,1,0:T(2,128)} %occ_m.1, ...), custom_call_target="tpu_custom_call" | custom-call | tf_op jit(solution)/shard_map/pallas_call | solution.py:520
  38.4 0.7 %copy.13 = f32[8,32,128]{2,1,0:T(8,128)} copy(f32[8,32,128]{2,1,0:T(8,128)S(1)} %get-tuple-element.3) | data formatting | bytes 262144
  39.1 0.7 %copy.14 = f32[16,16,256]{2,1,0:T(8,128)} copy(f32[16,16,256]{2,1,0:T(8,128)S(1)} %get-tuple-element.4) | data formatting | bytes 524288
  39.8 1.0 %copy.15 = f32[32,32,256]{2,1,0:T(8,128)} copy(f32[32,32,256]{2,1,0:T(8,128)S(1)} %get-tuple-element.5) | data formatting | bytes 2097152
where the time goes:
time: 41.3 us; the launch traced here: 40.7 us
  Pallas kernels  37.8 us (92%)
  local copies, waits for them, and re-layouts  2.33 us (6%)
  between operations  0.64 us (2%)
    pallas_call x1, Pallas kernels, shards(): pl.pallas_call(functools.partial(kernel, dims), out_shape=[pltpu.VMEM(a.s...  37.8 us
    unnamed x3, local copies, waits for them, and re-layouts  2.33 us

commit v1 on v0

v1 whole, which is shorter than its diff:
```python
import functools
import math

import jax
import jax.numpy as jnp
from jax import lax
from jax.experimental import pallas as pl
from jax.experimental.pallas import tpu as pltpu
from jax.sharding import PartitionSpec as P

MESH = pl.DeviceIdType.MESH
F32 = jnp.float32
BF16 = jnp.bfloat16
PAD = 4
ROWS = 8
LANES = 128
VMEM_BYTES = 67043328


def iota(shape, dim):
    return lax.broadcasted_iota(jnp.int32, shape, dim)


def logical(index, own, extra):
    if extra == 0:
        return index
    return jnp.where(index < own + extra // 2, index, index - (own + extra))


def prolong_matrix(fine, coarse, total):
    base = lax.shift_right_arithmetic(fine, 1)
    beside = base + 2 * (fine & 1) - 1
    inside = jnp.logical_and(fine >= 0, fine < total)
    value = jnp.where(coarse == base, 0.75, jnp.where(coarse == beside, 0.25, 0.0))
    return jnp.where(inside, value, 0.0).astype(BF16)


def split(values):
    high = values.astype(BF16)
    return high, (values - high.astype(F32)).astype(BF16)


def mm(a, b):
    return jnp.dot(a, b, preferred_element_type=F32)


def fold_rows(values):
    total = values[0:ROWS]
    for row in range(ROWS, values.shape[0], ROWS):
        total = total + values[row : row + ROWS]
    out = total[:, 0:LANES]
    for lane in range(LANES, values.shape[1], LANES):
        out = out + total[:, lane : lane + LANES]
    return out


def coefficients(m0, n1, n2, n3):
    rho = n1 / m0
    spread = n2 - rho * n1
    bent = 6.0 * spread + (n3 - 2.0 * rho * n2 + rho * rho * n1)
    turn = jnp.where(bent > 0.0, jnp.maximum(spread, 0.0) / bent, 0.0)
    first = m0 / ((6.0 + rho) * m0 - jnp.maximum(spread, 0.0) * turn)
    second = -first * turn
    return first - second * rho, second


def kernel(
    dims,
    rhs_c, rhs_m, rhs_f, occ_c, occ_m, occ_f, weight_in,
    out_c, out_m, fg, fr, fw, tg, tr, tw, coef,
    in_c, in_m, in_f, io_c, io_m, io_f, weight, isem,
    cr, cw, cs, cx, ctz, ct, oc,
    mb, mg, mr, mw, ms, mx, mtz, mt, om, m_up, m_dn, m_fu, m_fd, om_l, om_r,
    fb, fs, of, zsend, edge, f_up, f_dn, f_fu, f_fd, of_l, of_r,
    ac, am, af, ss, rs, sc, rc, sm, rm, sf, rf,
):
    nx, ny, nz = dims
    ix, iy, iz = lax.axis_index("gx"), lax.axis_index("gy"), lax.axis_index("gz")
    xc, yc, zc = rhs_c.shape
    xm, ym, zm = rhs_m.shape
    xf, yf, zh = rhs_f.shape
    zf = zh * nz
    xc, xm, xf = xc // nz, xm // nz, xf // nz
    slab = ix * nz + iz
    slabs = nx * nz
    bc, bm, bf = occ_c.shape, occ_m.shape, occ_f.shape
    x_low, x_high = ix > 0, ix < nx - 1
    y_low, y_high = iy > 0, iy < ny - 1
    lower, upper = iz == 0, iz == 1
    first, last = slab == 0, slab == slabs - 1

    def both(a, b):
        return jnp.logical_and(a, b)

    def at(offset):
        return (
            lax.rem(ix + offset[0], nx), lax.rem(iy + offset[1], ny), lax.rem(iz + offset[2], nz)
        )

    for ref in (oc, om, of):
        ref[...] = jnp.zeros_like(ref)

    barrier = pltpu.get_barrier_semaphore()
    peers = [(a, b, c) for a in range(nx) for b in range(ny) for c in range(nz)][1:]
    for offset in peers:
        pl.semaphore_signal(barrier, inc=1, device_id=at(offset), device_id_type=MESH)

    loads = {}
    pairs = (
        ("c", rhs_c, in_c), ("oc", occ_c, io_c), ("w", weight_in, weight), ("f", rhs_f, in_f),
        ("m", rhs_m, in_m), ("om", occ_m, io_m), ("of", occ_f, io_f),
    )
    for k, (name, src, dst) in enumerate(pairs):
        loads[name] = pltpu.make_async_copy(src, dst, isem.at[k])
        loads[name].start()

    @pl.when(first)
    def _():
        cr[0:4] = jnp.zeros((4, yc, zc), F32)
        mb[1:4, 0:ym, :] = jnp.zeros((3, ym, zm), F32)
        fb[2:4, 0:yf, :] = jnp.zeros((2, yf, zf), F32)

    @pl.when(last)
    def _():
        cr[PAD + xc : PAD + xc + 4] = jnp.zeros((4, yc, zc), F32)
        mb[PAD + xm : PAD + xm + 3, 0:ym, :] = jnp.zeros((3, ym, zm), F32)
        fb[PAD + xf : PAD + xf + 2, 0:yf, :] = jnp.zeros((2, yf, zf), F32)

    @pl.when(jnp.logical_not(x_low))
    def _():
        for ref in (om_l, om_r, of_l, of_r):
            ref[0:1] = jnp.zeros((1,) + tuple(ref.shape[1:]), F32)

    @pl.when(jnp.logical_not(x_high))
    def _():
        for ref in (om_l, om_r, of_l, of_r):
            size = ref.shape[0]
            ref[size - 1 : size] = jnp.zeros((1,) + tuple(ref.shape[1:]), F32)

    @pl.when(jnp.logical_not(y_low))
    def _():
        for ref in (m_fu, f_fu, om_l, of_l):
            ref[...] = jnp.zeros_like(ref)

    @pl.when(jnp.logical_not(y_high))
    def _():
        for ref in (m_fd, f_fd, om_r, of_r):
            ref[...] = jnp.zeros_like(ref)

    loads["c"].wait()
    cr[pl.ds(PAD - 4 * iz, xc + 4)] = in_c[pl.ds(iz * (xc - 4), xc + 4)].astype(F32)
    loads["oc"].wait()
    oc[1 : 1 + bc[0], 0 : bc[1], 0 : bc[2]] = io_c[...].astype(F32)

    pl.semaphore_wait(barrier, len(peers))

    used = [0]

    def copy(src, dst, target, step=0, count=1):
        k = used[0]
        used[0] += count
        made = [
            pltpu.make_async_remote_copy(
                src_ref=src, dst_ref=dst, send_sem=ss.at[k], recv_sem=rs.at[k + j],
                device_id=target, device_id_type=MESH,
            )
            for j in range(count)
        ]
        if count == 1:
            return made[0]
        sender = pltpu.make_async_remote_copy(
            src_ref=src, dst_ref=dst, send_sem=ss.at[k], recv_sem=rs.at[k + step],
            device_id=target, device_id_type=MESH,
        )
        return sender, made

    def start(items):
        for c, can_send, _ in items:
            if can_send is None:
                c.start()
            elif can_send is not False:
                pl.when(can_send)(c.start)

    def arrive(items):
        for c, _, can_recv in items:
            if can_recv is None:
                c.wait_recv()
            elif can_recv is not False:
                pl.when(can_recv)(c.wait_recv)

    def left(items):
        for c, can_send, _ in items:
            if can_send is None:
                c.wait_send()
            elif can_send is not False:
                pl.when(can_send)(c.wait_send)

    above, below = {"gx": ix + 1, "gz": 0}, {"gx": ix - 1, "gz": 1}
    send_up, get_low = both(upper, x_high), both(lower, x_low)
    send_down, get_high = both(lower, x_low), both(upper, x_high)

    def slab_swap(ref, own, rows, width_low, width_high, skip_low=0, skip_high=0):
        items = []
        stop = PAD + own - skip_low
        items.append((copy(ref.at[stop - width_low : stop, 0:rows, :],
                           ref.at[PAD - skip_low - width_low : PAD - skip_low, 0:rows, :], above),
                      send_up, get_low))
        begin = PAD + skip_high
        items.append((copy(ref.at[begin : begin + width_high, 0:rows, :],
                           ref.at[begin + own : begin + own + width_high, 0:rows, :], below),
                      send_down, get_high))
        return items

    def x_flags(occ, bricks):
        return [
            (copy(occ.at[bricks], occ.at[0], {"gx": ix + 1}), x_high, x_low),
            (copy(occ.at[1], occ.at[bricks + 1], {"gx": ix - 1}), x_low, x_high),
        ]

    def y_flags(occ, occ_l, occ_r, bricks):
        items = []
        flags = pl.ds(1, bricks)
        for dst, step, can_send, can_recv in (
            (occ_l, 1, y_high, y_low), (occ_r, -1, y_low, y_high)
        ):
            items.append((copy(occ.at[flags], dst.at[flags], {"gy": iy + step}), can_send, can_recv))
            items.append((copy(occ.at[bricks], dst.at[0], {"gx": ix + 1, "gy": iy + step}),
                          both(can_send, x_high), both(can_recv, x_low)))
            items.append((copy(occ.at[1], dst.at[bricks + 1], {"gx": ix - 1, "gy": iy + step}),
                          both(can_send, x_low), both(can_recv, x_high)))
        return items

    def y_swap(ref, own, rows, width, low, high, to_up, to_down, from_low, from_high):
        span = slice(PAD - low, PAD + own + high)
        to_up[...] = ref[span, rows - width : rows, :]
        to_down[...] = ref[span, 0:width, :]
        return [
            (copy(to_up, from_low, {"gy": iy + 1}), y_high, y_low),
            (copy(to_down, from_high, {"gy": iy - 1}), y_low, y_high),
        ]

    def y_merge(ref, own, width, from_low, from_high, begin):
        count = from_low.shape[0]
        parts = [from_high[...], from_low[...]]
        if 2 * width < ROWS:
            parts.insert(1, jnp.zeros((count, ROWS - 2 * width, ref.shape[2]), F32))
        ref[begin : begin + count, own : own + ROWS, :] = jnp.concatenate(parts, axis=1)

    near = slab_swap(cr, xc, yc, 1, 2) + x_flags(oc, bc[0])
    start(near)
    far = slab_swap(cr, xc, yc, 3, 2, 1, 2)
    start(far)

    loads["f"].wait()
    own_z = pl.ds(pl.multiple_of(iz * zh, LANES), zh)
    other = 1 - iz

    def fill_fine(j, carry):
        zsend[j] = in_f[other * (xf - 2) + j].astype(F32)
        fb[PAD - 2 * iz + j, 0:yf, own_z] = in_f[iz * (xf - 2) + j].astype(F32)
        return carry

    lax.fori_loop(0, xf + 2, fill_fine, 0)
    loads["of"].wait()
    own_flags = pl.ds(pl.multiple_of(iz * LANES, LANES), LANES)
    flags = jnp.concatenate(
        [io_f[...].astype(F32), jnp.zeros((bf[0], bf[1], LANES - bf[2]), F32)], axis=2
    )
    of[1 : 1 + bf[0], 0 : bf[1], own_flags] = flags
    partner = {"gz": other}
    z_fine = [
        (copy(zsend, fb.at[pl.ds(PAD - 2 * other, xf + 2), 0:yf, own_z], partner), None, None),
        (copy(of.at[pl.ds(1, bf[0]), :, own_flags], of.at[pl.ds(1, bf[0]), :, own_flags], partner),
         None, None),
    ]
    start(z_fine)

    loads["m"].wait()
    mb[pl.ds(PAD - 3 * iz, xm + 3), 0:ym, :] = in_m[pl.ds(iz * (xm - 3), xm + 3)].astype(F32)
    loads["om"].wait()
    om[1 : 1 + bm[0], 0 : bm[1], 0 : bm[2]] = io_m[...].astype(F32)
    mid_x = slab_swap(mb, xm, ym, 3, 3)
    start(mid_x)
    mid_flags = x_flags(om, bm[0]) + y_flags(om, om_l, om_r, bm[0])
    start(mid_flags)
    edge[0:2] = in_f[0:2].astype(F32)
    edge[2] = in_f[nz * xf - 1].astype(F32)

    def row_prolong(own, extra, index, total, cols, col_own, col_extra, col_index):
        shape = (own + extra, cols)
        fine = logical(iota(shape, 0), own, extra) + own * index
        coarse = logical(iota(shape, 1), col_own, col_extra) + col_own * col_index
        return prolong_matrix(fine, coarse, total)

    def lane_prolong(cells, rows):
        shape = (rows, cells)
        return prolong_matrix(iota(shape, 1), iota(shape, 0), cells)

    def lane_bricks(cells, bricks, halves):
        shape = (halves * LANES, cells)
        brick = lax.div(iota(shape, 1), cells // (bricks * halves))
        place = brick + lax.div(brick, bricks) * (LANES - bricks)
        return (place == iota(shape, 0)).astype(BF16)

    def screens(dest, occ_parts, own, extra_rows, bricks_y, lane_matrix, level):
        count = dest.shape[0]
        side = own // bricks_y
        cols = ROWS * len(occ_parts)
        shape = (dest.shape[1], cols)
        brick = lax.div(logical(iota(shape, 0), own, extra_rows) + side, side) - 1
        place = jnp.where(
            brick < 0, ROWS + bricks_y - 1, jnp.where(brick >= bricks_y, 2 * ROWS, brick)
        )
        row_matrix = (place == iota(shape, 1)).astype(BF16)
        for x in range(count):
            flags = jnp.concatenate([part[x] for part in occ_parts], axis=0).astype(BF16)
            wide = mm(flags, lane_matrix).astype(BF16)
            dest[x] = weight[level] * (0.25 + mm(row_matrix, wide))

    def along_y(v):
        n = v.shape[0]
        return pltpu.roll(v, 1, 0), pltpu.roll(v, n - 1, 0)

    def z_up(v):
        n = v.shape[1]
        turned = pltpu.roll(v, 1, 1)
        edge_lane = iota((v.shape[0], LANES), 1) == 0
        fixed = jnp.where(edge_lane, 0.0, turned[:, 0:LANES])
        return fixed if n == LANES else jnp.concatenate([fixed, turned[:, LANES:]], axis=1)

    def z_down(v):
        n = v.shape[1]
        turned = pltpu.roll(v, n - 1, 1)
        edge_lane = iota((v.shape[0], LANES), 1) == LANES - 1
        fixed = jnp.where(edge_lane, 0.0, turned[:, n - LANES :])
        return fixed if n == LANES else jnp.concatenate([turned[:, : n - LANES], fixed], axis=1)

    loads["w"].wait()
    lanes_c = lane_bricks(zc, bc[2], 1)
    side_c = nz * xc // bc[0]
    shape_c = (yc, zc)
    row_c = iota(shape_c, 0)

    def sum_c(v, twice):
        yu, yd = along_y(v)
        total = jnp.where(row_c < yc - 1, yd, 0.0) + z_down(v)
        if twice:
            total = total + jnp.where(row_c > 0, yu, 0.0) + z_up(v)
        return total

    def brick_of(own, side):
        return lambda p: lax.div(own * iz + p + (side - PAD), side)

    brick_c = brick_of(xc, side_c)

    def coarse_w(p, carry):
        r = cr[p]
        place = xc * slab + p - PAD
        keep = both(place >= 0, place < xc * slabs).astype(F32)
        screen = cs[brick_c(p)]
        cw[p] = keep * (screen * r - (cr[p - 1] + cr[p + 1] + sum_c(r, True)))
        return carry

    def coarse_moments(p, acc):
        r, w = cr[p], cw[p]
        image = cs[brick_c(p)] * w - 2.0 * (cw[p + 1] + sum_c(w, False))
        return tuple(a + fold_rows(b) for a, b in zip(acc, (r * r, r * w, w * w, w * image)))

    zero = jnp.zeros((ROWS, LANES), F32)
    lane_index = iota((1, LANES), 1)

    def spread_moments(acc, buf, send, recv, offsets, slot):
        row = jnp.zeros((1, LANES), F32)
        for k, a in enumerate(acc):
            value = jnp.sum(jnp.sum(a, axis=0, keepdims=True), axis=1, keepdims=True)
            row = jnp.where(lane_index == k, value, row)
        buf[slot] = row
        copies = []
        for k, offset in enumerate(offsets):
            c = pltpu.make_async_remote_copy(
                src_ref=buf.at[slot], dst_ref=buf.at[slot], send_sem=send.at[k],
                recv_sem=recv.at[k], device_id=at(offset), device_id_type=MESH,
            )
            c.start()
            copies.append(c)
        return copies

    def solve(copies, buf):
        for c in copies:
            c.wait_recv()
        total = [buf[k] for k in range(buf.shape[0])]
        while len(total) > 1:
            total = [sum(total[k : k + 2][1:], total[k]) for k in range(0, len(total), 2)]
        return coefficients(*[
            jnp.sum(jnp.where(lane_index == k, total[0], 0.0), axis=1, keepdims=True)
            for k in range(4)
        ])

    flat_slot = (ix * ny + iy) * nz + iz
    arrive(near)
    screens(cs, [oc], yc, 0, bc[1], lanes_c, 0)
    lax.fori_loop(PAD, PAD + xc + 1, coarse_w, 0, unroll=True)
    acc = lax.fori_loop(PAD, PAD + xc, coarse_moments, (zero,) * 4, unroll=True)
    coarse_copies = spread_moments(acc, ac, sc, rc, [o for o in peers if o[1] == 0], slab)

    pair_up, made_up = copy(
        edge.at[pl.ds(2, 1)], fb.at[pl.ds(PAD - 1, 1), 0:yf, own_z], above, iz, nz
    )
    pair_dn, made_dn = copy(
        edge.at[pl.ds(0, 2)], fb.at[pl.ds(PAD + xf, 2), 0:yf, own_z], below, iz, nz
    )
    fine_x = [(pair_up, x_high, False), (pair_dn, x_low, False)]
    fine_x += [(c, False, get_low) for c in made_up] + [(c, False, get_high) for c in made_dn]
    start(fine_x)

    arrive(mid_x)
    mid_y = y_swap(mb, xm, ym, 4, 3, 3, m_up, m_dn, m_fu, m_fd)
    start(mid_y)
    arrive(far)
    lax.fori_loop(1, PAD, coarse_w, 0, unroll=True)
    lax.fori_loop(PAD + xc + 1, PAD + xc + 3, coarse_w, 0, unroll=True)
    mid_lanes = lane_prolong(zm, zc)
    mid_rows = row_prolong(ym, ROWS, iy, ym * ny, yc, yc, 0, 0)
    arrive(z_fine)
    fine_flags = x_flags(of, bf[0]) + y_flags(of, of_l, of_r, bf[0])
    start(fine_flags)
    arrive(mid_flags)
    lanes_m = lane_bricks(zm, bm[2], 1)
    screens(ms, [om, om_l, om_r], ym, ROWS, bm[1], lanes_m, 1)

    ka, kb = solve(coarse_copies, ac)
    for j in range(xc + 6):
        cx[j] = ka * cr[j + 1] + kb * cw[j + 1]
    own_c = pl.ds(iz * xc, xc)
    out_c[own_c] = cx[3 : 3 + xc]
    outs = [(copy(out_c.at[own_c], out_c.at[own_c], partner), None, None)]
    start(outs)

    def prolong(src, tz, dst, lane_matrix, row_matrix):
        n, rows, lanes = src.shape
        high, low = split(src[...].reshape(n * rows, lanes))
        tz[...] = (mm(high, lane_matrix) + mm(low, lane_matrix)).reshape(tz.shape)
        for j in range(n):
            high, low = split(tz[j])
            dst[j] = mm(row_matrix, high) + mm(row_matrix, low)

    def interpolate(t, g, own, begin, low, high):
        for p in range(PAD - low, PAD + own + high):
            m = p - PAD
            j = m // 2
            beside = min(max(j + (1 if m % 2 else -1) - begin, 0), t.shape[0] - 1)
            if 0 <= m < own:
                g[p] = 0.75 * t[j - begin] + 0.25 * t[beside]
            else:
                place = own * slab + m
                keep = both(place >= 0, place < own * slabs).astype(F32)
                g[p] = (0.75 * keep) * t[j - begin] + (0.25 * keep) * t[beside]

    def neighbours(v):
        yu, yd = along_y(v)
        return yu + yd + z_up(v) + z_down(v)

    def clear(ref, own, low, high):
        empty = jnp.zeros(ref.shape[1:], F32)

        @pl.when(first)
        def _():
            for p in range(PAD - low, PAD):
                ref[p] = empty

        @pl.when(last)
        def _():
            for p in range(PAD + own, PAD + own + high):
                ref[p] = empty

    def run_depth(b, g, r, w, s, own, rows, index, total, side, r_low, r_high, unroll):
        brick = brick_of(own, side)
        shape = (ROWS, b.shape[2])
        row = logical(iota(shape, 0) + rows, rows, ROWS) + rows * index
        mask = both(row >= 0, row < total).astype(F32)

        def masked(v):
            return jnp.concatenate([v[0:rows], v[rows:] * mask], axis=0)

        def make_r(p, carry):
            c = g[p]
            value = b[p] - (6.0 + s[brick(p)]) * c
            r[p] = masked(value + (g[p - 1] + g[p + 1]) + neighbours(c))
            return carry

        lax.fori_loop(PAD - r_low, PAD + own + r_high, make_r, 0, unroll=unroll)
        clear(r, own, r_low, r_high)

        def make_w(p, carry):
            c = r[p]
            w[p] = masked(s[brick(p)] * c - (r[p - 1] + r[p + 1]) - neighbours(c))
            return carry

        lax.fori_loop(PAD - r_low + 1, PAD + own + r_high - 1, make_w, 0, unroll=unroll)
        clear(w, own, r_low - 1, r_high - 1)

        def moments(p, acc):
            rv, full = r[p, 0:rows], w[p]
            wv = full[0:rows]
            image = s[brick(p), 0:rows] * wv - 2.0 * (
                w[p + 1, 0:rows] + along_y(full)[1][0:rows] + z_down(wv)
            )
            return tuple(
                a + fold_rows(v) for a, v in zip(acc, (rv * rv, rv * wv, wv * wv, wv * image))
            )

        return lax.fori_loop(PAD, PAD + own, moments, (zero,) * 4, unroll=unroll)

    prolong(cx, ctz, ct, mid_lanes, mid_rows)
    interpolate(ct, mg, xm, -3, 4, 4)
    arrive(mid_y)
    y_merge(mb, ym, 4, m_fu, m_fd, 1)
    acc = run_depth(mb, mg, mr, mw, ms, xm, ym, iy, ym * ny, nz * xm // bm[0], 3, 3, 2)
    mid_copies = spread_moments(acc, am, sm, rm, peers, flat_slot)

    arrive(fine_x)
    fine_y = y_swap(fb, xf, yf, 2, 1, 2, f_up, f_dn, f_fu, f_fd)
    start(fine_y)
    arrive(fine_flags)
    lanes_f = lane_bricks(zf, bf[2], nz)
    screens(fs, [of, of_l, of_r], yf, ROWS, bf[1], lanes_f, 2)
    fine_lanes = lane_prolong(zf, zm)
    fine_rows = row_prolong(yf, ROWS, iy, yf * ny, ym + ROWS, ym, ROWS, iy)
    arrive(fine_y)
    y_merge(fb, yf, 2, f_fu, f_fd, PAD - 1)
    ka, kb = solve(mid_copies, am)
    for p in range(2, xm + 6):
        mx[p - 2] = mg[p] + ka * mr[p] + kb * mw[p]
    own_m = pl.ds(iz * xm, xm)
    out_m[own_m] = mx[2 : 2 + xm, 0:ym, :]
    outs.append((copy(out_m.at[own_m], out_m.at[own_m], partner), None, None))
    start(outs[1:])

    prolong(mx, mtz, mt, fine_lanes, fine_rows)
    interpolate(mt, fg, xf, -2, 2, 3)
    acc = run_depth(fb, fg, fr, fw, fs, xf, yf, iy, yf * ny, nz * xf // bf[0], 1, 2, 2)
    fine_copies = spread_moments(acc, af, sf, rf, peers, flat_slot)
    their_z = pl.ds(pl.multiple_of(other * zh, LANES), zh)
    back = [
        (copy(src.at[PAD : PAD + xf, 0:yf, their_z], dst, partner), None, None)
        for src, dst in ((fg, tg), (fr, tr), (fw, tw))
    ]
    start(back)
    for items in (near, far, z_fine, mid_x, mid_flags, fine_x, mid_y, fine_flags, fine_y, outs):
        left(items)
    for c in coarse_copies + mid_copies:
        c.wait_send()
    arrive(outs)
    arrive(back)
    left(back)
    ka, kb = solve(fine_copies, af)
    coef[0] = jnp.broadcast_to(ka, (ROWS, LANES))
    coef[1] = jnp.broadcast_to(kb, (ROWS, LANES))
    for c in fine_copies:
        c.wait_send()


def finish(g, r, w, tg, tr, tw, coef, sol_c, sol_m, out_c, out_m, out_f, buf, sem):
    iz = lax.axis_index("gz")
    xs, yf, zh = tg.shape
    small = [
        pltpu.make_async_copy(sol_c, out_c, sem.at[0]),
        pltpu.make_async_copy(sol_m, out_m, sem.at[1]),
    ]
    for c in small:
        c.start()
    own_z = pl.ds(pl.multiple_of(iz * zh, LANES), zh)
    ka, kb = coef[0, 0:1, 0:1], coef[1, 0:1, 0:1]
    parts = 2
    step = xs // parts
    copies = list(small)
    for part in range(parts):
        for side in range(2):
            place = (iz if side == 0 else 1 - iz) * xs

            def one(x, carry):
                if side == 0:
                    p = x + PAD
                    value = g[p, 0:yf, own_z] + ka * r[p, 0:yf, own_z] + kb * w[p, 0:yf, own_z]
                else:
                    value = tg[x] + ka * tr[x] + kb * tw[x]
                buf[place + x] = value
                return carry

            lax.fori_loop(part * step, part * step + step, one, 0, unroll=2)
            span = pl.ds(place + part * step, step)
            c = pltpu.make_async_copy(buf.at[span], out_f.at[span], sem.at[2 + 2 * part + side])
            c.start()
            copies.append(c)
    for c in copies:
        c.wait()


def shards(dims, *args):
    nx, ny, nz = dims
    rhs_c, rhs_m, rhs_f, occ_c, occ_m, occ_f, _ = args
    xc, yc, zc = rhs_c.shape
    xm, ym, zm = rhs_m.shape
    xf, yf, zh = rhs_f.shape
    zf = zh * nz
    xc, xm, xf = xc // nz, xm // nz, xf // nz
    me, fe = (ym + ROWS, zm), (yf + ROWS, zf)

    def buf(*shape):
        return pltpu.VMEM(shape, F32)

    bm, bf = occ_m.shape[0] + 2, occ_f.shape[0] + 2
    scratch = [
        pltpu.VMEM(a.shape, a.dtype) for a in (rhs_c, rhs_m, rhs_f, occ_c, occ_m, occ_f)
    ]
    scratch += [pltpu.SMEM(args[6].shape, F32), pltpu.SemaphoreType.DMA((7,))]
    scratch += [
        buf(xc + 8, yc, zc), buf(xc + 8, yc, zc), buf(occ_c.shape[0] + 2, yc, zc),
        buf(xc + 6, yc, zc), buf(xc + 6, yc, zm), buf(xc + 6, *me),
        buf(occ_c.shape[0] + 2, ROWS, LANES),
        buf(xm + 8, *me), buf(xm + 8, *me), buf(xm + 8, *me), buf(xm + 8, *me), buf(bm, *me),
        buf(xm + 4, *me), buf(xm + 4, me[0], zf), buf(xm + 4, *fe),
        buf(bm, ROWS, LANES),
        buf(xm + 6, 4, zm), buf(xm + 6, 4, zm), buf(xm + 6, 4, zm), buf(xm + 6, 4, zm),
        buf(bm, ROWS, LANES), buf(bm, ROWS, LANES),
        buf(xf + 8, *fe), buf(bf, *fe), buf(bf, ROWS, nz * LANES),
        buf(xf + 2, yf, zh), buf(3, yf, zh),
        buf(xf + 3, 2, zf), buf(xf + 3, 2, zf), buf(xf + 3, 2, zf), buf(xf + 3, 2, zf),
        buf(bf, ROWS, nz * LANES), buf(bf, ROWS, nz * LANES),
        buf(nx * nz, 1, LANES), buf(nx * ny * nz, 1, LANES), buf(nx * ny * nz, 1, LANES),
    ]
    for count in (48, nx * nz, nx * ny * nz, nx * ny * nz):
        scratch += [pltpu.SemaphoreType.DMA((count,))] * 2
    hbm = pl.BlockSpec(memory_space=pltpu.HBM)
    vmem = pl.BlockSpec(memory_space=pltpu.VMEM)
    field = pltpu.VMEM((xf + 8,) + fe, F32)
    half = pltpu.VMEM((xf, yf, zh), F32)
    made_shapes = [pltpu.VMEM(a.shape, F32) for a in args[:2]]
    made_shapes += [field] * 3 + [half] * 3 + [pltpu.VMEM((2, ROWS, LANES), F32)]
    room = sum(4 * math.prod(a.shape) for a in made_shapes)
    made = pl.pallas_call(
        functools.partial(kernel, dims),
        out_shape=made_shapes,
        in_specs=[hbm] * 7,
        out_specs=[vmem] * 9,
        scratch_shapes=scratch,
        compiler_params=pltpu.CompilerParams(
            collective_id=0, has_side_effects=True, vmem_limit_bytes=VMEM_BYTES - room
        ),
    )(*args)
    sol_c, sol_m, fields = made[0], made[1], made[2:]
    return pl.pallas_call(
        finish,
        out_shape=[jax.ShapeDtypeStruct(a.shape, F32) for a in args[:3]],
        in_specs=[vmem] * 9,
        out_specs=[hbm] * 3,
        scratch_shapes=[pltpu.VMEM(rhs_f.shape, F32), pltpu.SemaphoreType.DMA((6,))],
        compiler_params=pltpu.CompilerParams(vmem_limit_bytes=16 * 1024 * 1024),
    )(*fields, sol_c, sol_m)


def solution(mesh):
    dims = tuple(mesh.shape[axis] for axis in ("gx", "gy", "gz"))
    in_specs = (
        P("gx", None, None), P("gx", "gy", None), P("gx", "gy", "gz"),
        P("gx", None, None), P("gx", "gy", None), P("gx", "gy", "gz"), P(),
    )
    out_specs = (P("gx", None, None), P("gx", "gy", None), P("gx", "gy", "gz"))
    return jax.shard_map(
        functools.partial(shards, dims), mesh=mesh, in_specs=in_specs, out_specs=out_specs,
        check_vma=False,
    )
```

time: 41.3 us -> 34.5 us (0.84); the launches traced: 40.7 us -> 34.4 us
  Pallas kernels: 37.8 us -> 33.7 us
  local copies, waits for them, and re-layouts: 2.33 us -> 0 us
    pallas_call x1 -> x2, Pallas kernels: 37.8 us -> 33.7 us  [the longest x1 32.5 us: shards(): pl.pallas_call(functools.partial(kernel, dims), out_shape=made_shapes, in...]
    unnamed x3 -> x0, local copies, waits for them, and re-layouts: 2.33 us -> none
where the time goes in v1:
time: 34.5 us; the launch traced here: 34.4 us
  Pallas kernels  33.7 us (98%)
  between operations  0.64 us (2%)
    pallas_call x1, Pallas kernels, shards(): pl.pallas_call(functools.partial(kernel, dims), out_shape=made_shapes, in...  32.5 us
    pallas_call x1, Pallas kernels, shards(): pl.pallas_call(finish, out_shape=[jax.ShapeDtypeStruct(a.shape, F32) for...  1.2 us

profile of v1, /device:TPU:0, one launch (start us, length us, event | category | flops | bytes accessed | tf_op | source)
XLA Modules:
  0.0 34.4 jit_solution(17779472293997478083)
XLA Ops:
  0.6 32.5 %shard_map.94 = (f32[8,32,128]{2,1,0:T(8,128)S(1)}, f32[16,16,256]{2,1,0:T(8,128)S(1)}, f32[24,40,512]{2,1,0:T(8,128)S(1)}, f32[24,40,512]{2,1,0:T(8,128)S(1)}, ...) custom-call(bf16[8,32,128]{2,1,0:T(8,128)(2,1)} %rhs_c.1, ...), custom_call_target="tpu_custom_call" | custom-call | tf_op jit(solution)/shard_map/pallas_call | solution.py:641
  33.2 1.2 %shard_map.95 = (f32[8,32,128]{2,1,0:T(8,128)}, f32[16,16,256]{2,1,0:T(8,128)}, f32[32,32,256]{2,1,0:T(8,128)}) custom-call(f32[24,40,512]{2,1,0:T(8,128)S(1)} %get-tuple-element.12.g, f32[24,40,512]{2,1,0:T(8,128)S(1)} %get-tuple-element.13.r, f32[24,40,512]{2,1,0:T(8,128)S(1)} %get-tuple-element.14.w, f32[16,32,256]{2,1,0:T(8,128)S(1)} %get-tuple-element.15.tg, ...), custom_call_target="tpu_custom_call" | custom-call | tf_op jit(solution)/shard_map/pallas_call | solution.py:652

commit v2 on v1

--- a/solution.py
+++ b/solution.py
@@ -15,6 +15,7 @@
 ROWS = 8
 LANES = 128
 VMEM_BYTES = 67043328
+UNROLL = 2
 
 
 def iota(shape, dim):
@@ -69,10 +70,10 @@
     rhs_c, rhs_m, rhs_f, occ_c, occ_m, occ_f, weight_in,
     out_c, out_m, fg, fr, fw, tg, tr, tw, coef,
     in_c, in_m, in_f, io_c, io_m, io_f, weight, isem,
-    cr, cw, cs, cx, ctz, ct, oc,
-    mb, mg, mr, mw, ms, mx, mtz, mt, om, m_up, m_dn, m_fu, m_fd, om_l, om_r,
+    cr, cw, cs, ctz, ct, oc,
+    mb, g1, g2, u1, u2, v0, v1, v2, ms, mx, mtz, mt, om, m_up, m_dn, m_fu, m_fd, om_l, om_r,
     fb, fs, of, zsend, edge, f_up, f_dn, f_fu, f_fd, of_l, of_r,
-    ac, am, af, ss, rs, sc, rc, sm, rm, sf, rf,
+    am, af, ss, rs, sm, rm, sf, rf, relay,
 ):
     nx, ny, nz = dims
     ix, iy, iz = lax.axis_index("gx"), lax.axis_index("gy"), lax.axis_index("gz")
@@ -102,8 +103,40 @@
 
     barrier = pltpu.get_barrier_semaphore()
     peers = [(a, b, c) for a in range(nx) for b in range(ny) for c in range(nz)][1:]
-    for offset in peers:
-        pl.semaphore_signal(barrier, inc=1, device_id=at(offset), device_id_type=MESH)
+    around = [(a, b) for a in (-1, 1, 0) for b in (-1, 1, 0)]
+
+    def exists(a, b):
+        there = [c for c, step in ((x_low, a == -1), (x_high, a == 1), (y_low, b == -1), (y_high, b == 1)) if step]
+        return functools.reduce(both, there) if there else None
+
+    def greet(semaphore, a, b, c):
+        target = (ix + a, iy + b, c)
+
+        def send():
+            pl.semaphore_signal(semaphore, inc=1, device_id=target, device_id_type=MESH)
+
+        there = exists(a, b)
+        if there is None:
+            send()
+        else:
+            pl.when(there)(send)
+
+    for a, b in around:
+        for c in range(1 if (a, b) == (0, 0) else 0, nz):
+            greet(barrier, a, b, lax.rem(iz + c, nz))
+    chips = (1 + jnp.where(x_low, 1, 0) + jnp.where(x_high, 1, 0)) * (
+        1 + jnp.where(y_low, 1, 0) + jnp.where(y_high, 1, 0)
+    )
+    rounds = max(nx, ny) - 2
+
+    def relay_send(k):
+        if k < rounds:
+            for a, b in around[:-1]:
+                greet(relay.at[k], a, b, iz)
+
+    def relay_wait(k):
+        if k < rounds:
+            pl.semaphore_wait(relay.at[k], chips - 1)
 
     loads = {}
     pairs = (
@@ -117,12 +150,18 @@
     @pl.when(first)
     def _():
         cr[0:4] = jnp.zeros((4, yc, zc), F32)
+        cs[0] = jnp.zeros((yc, zc), F32)
+        for ref in (m_fu, m_fd):
+            ref[0:3] = jnp.zeros((3,) + tuple(ref.shape[1:]), F32)
         mb[1:4, 0:ym, :] = jnp.zeros((3, ym, zm), F32)
         fb[2:4, 0:yf, :] = jnp.zeros((2, yf, zf), F32)
 
     @pl.when(last)
     def _():
         cr[PAD + xc : PAD + xc + 4] = jnp.zeros((4, yc, zc), F32)
+        cs[bc[0] + 1] = jnp.zeros((yc, zc), F32)
+        for ref in (m_fu, m_fd):
+            ref[xm + 3 : xm + 6] = jnp.zeros((3,) + tuple(ref.shape[1:]), F32)
         mb[PAD + xm : PAD + xm + 3, 0:ym, :] = jnp.zeros((3, ym, zm), F32)
         fb[PAD + xf : PAD + xf + 2, 0:yf, :] = jnp.zeros((2, yf, zf), F32)
 
@@ -152,7 +191,8 @@
     loads["oc"].wait()
     oc[1 : 1 + bc[0], 0 : bc[1], 0 : bc[2]] = io_c[...].astype(F32)
 
-    pl.semaphore_wait(barrier, len(peers))
+    pl.semaphore_wait(barrier, chips * nz - 1)
+    relay_send(0)
 
     used = [0]
 
@@ -230,26 +270,88 @@
                           both(can_send, x_low), both(can_recv, x_high)))
         return items
 
-    def y_swap(ref, own, rows, width, low, high, to_up, to_down, from_low, from_high):
+    def y_swap(ref, own, rows, low, high, to_up, to_down, from_low, from_high):
         span = slice(PAD - low, PAD + own + high)
-        to_up[...] = ref[span, rows - width : rows, :]
-        to_down[...] = ref[span, 0:width, :]
+        to_up[...] = ref[span, rows - to_up.shape[1] : rows, :]
+        to_down[...] = ref[span, 0 : to_down.shape[1], :]
         return [
             (copy(to_up, from_low, {"gy": iy + 1}), y_high, y_low),
             (copy(to_down, from_high, {"gy": iy - 1}), y_low, y_high),
         ]
 
-    def y_merge(ref, own, width, from_low, from_high, begin):
+    def y_merge(ref, own, from_low, from_high, begin):
         count = from_low.shape[0]
         parts = [from_high[...], from_low[...]]
-        if 2 * width < ROWS:
-            parts.insert(1, jnp.zeros((count, ROWS - 2 * width, ref.shape[2]), F32))
+        gap = ROWS - from_low.shape[1] - from_high.shape[1]
+        if gap:
+            parts.insert(1, jnp.zeros((count, gap, ref.shape[2]), F32))
         ref[begin : begin + count, own : own + ROWS, :] = jnp.concatenate(parts, axis=1)
 
-    near = slab_swap(cr, xc, yc, 1, 2) + x_flags(oc, bc[0])
+    def row_prolong(own, extra, index, total, cols, col_own, col_extra, col_index):
+        shape = (own + extra, cols)
+        fine = logical(iota(shape, 0), own, extra) + own * index
+        coarse = logical(iota(shape, 1), col_own, col_extra) + col_own * col_index
+        return prolong_matrix(fine, coarse, total)
+
+    def lane_prolong(cells, rows):
+        shape = (rows, cells)
+        return prolong_matrix(iota(shape, 1), iota(shape, 0), cells)
+
+    def lane_bricks(cells, bricks, halves):
+        shape = (halves * LANES, cells)
+        brick = lax.div(iota(shape, 1), cells // (bricks * halves))
+        place = brick + lax.div(brick, bricks) * (LANES - bricks)
+        return (place == iota(shape, 0)).astype(BF16)
+
+    def screens(dest, begin, count, occ_parts, own, extra_rows, bricks_y, lane_matrix, level):
+        side = own // bricks_y
+        cols = ROWS * len(occ_parts)
+        shape = (dest.shape[1], cols)
+        brick = lax.div(logical(iota(shape, 0), own, extra_rows) + side, side) - 1
+        place = jnp.where(
+            brick < 0, ROWS + bricks_y - 1, jnp.where(brick >= bricks_y, 2 * ROWS, brick)
+        )
+        row_matrix = (place == iota(shape, 1)).astype(BF16)
+        flags = [part[begin + x] for x in range(count) for part in occ_parts]
+        wide = mm(jnp.concatenate(flags, axis=0).astype(BF16), lane_matrix).astype(BF16)
+        for x in range(count):
+            cells = mm(row_matrix, wide[x * cols : (x + 1) * cols])
+            dest[begin + x] = weight[level] * (0.25 + cells)
+
+    near = slab_swap(cr, xc, yc, 1, 2)
     start(near)
+    loads["w"].wait()
+    screens(cs, 1, bc[0], [oc], yc, 0, bc[1], lane_bricks(zc, bc[2], 1), 0)
+    near_screens = [
+        (copy(cs.at[bc[0]], cs.at[0], above), send_up, get_low),
+        (copy(cs.at[1], cs.at[bc[0] + 1], below), send_down, get_high),
+    ]
+    start(near_screens)
     far = slab_swap(cr, xc, yc, 3, 2, 1, 2)
     start(far)
+
+    loads["m"].wait()
+    mb[pl.ds(PAD - 3 * iz, xm + 3), 0:ym, :] = in_m[pl.ds(iz * (xm - 3), xm + 3)].astype(F32)
+    loads["om"].wait()
+    om[1 : 1 + bm[0], 0 : bm[1], 0 : bm[2]] = io_m[...].astype(F32)
+    mid_flags = x_flags(om, bm[0]) + y_flags(om, om_l, om_r, bm[0])
+    start(mid_flags)
+    mid_x = slab_swap(mb, xm, ym, 3, 3)
+    start(mid_x)
+    held = pl.ds(3 - 3 * iz, xm + 3)
+    m_up[held] = mb[pl.ds(PAD - 3 * iz, xm + 3), ym - 4 : ym, :]
+    m_dn[held] = mb[pl.ds(PAD - 3 * iz, xm + 3), 0:4, :]
+    mid_y = []
+    for src, dst, step, can_send, can_recv in (
+        (m_up, m_fu, 1, y_high, y_low), (m_dn, m_fd, -1, y_low, y_high)
+    ):
+        side = {"gy": iy + step}
+        mid_y.append((copy(src.at[held], dst.at[held], side), can_send, can_recv))
+        mid_y.append((copy(src.at[xm : xm + 3], dst.at[0:3], {**above, **side}),
+                      both(can_send, send_up), both(can_recv, get_low)))
+        mid_y.append((copy(src.at[3:6], dst.at[xm + 3 : xm + 6], {**below, **side}),
+                      both(can_send, send_down), both(can_recv, get_high)))
+    start(mid_y)
 
     loads["f"].wait()
     own_z = pl.ds(pl.multiple_of(iz * zh, LANES), zh)
@@ -275,134 +377,8 @@
     ]
     start(z_fine)
 
-    loads["m"].wait()
-    mb[pl.ds(PAD - 3 * iz, xm + 3), 0:ym, :] = in_m[pl.ds(iz * (xm - 3), xm + 3)].astype(F32)
-    loads["om"].wait()
-    om[1 : 1 + bm[0], 0 : bm[1], 0 : bm[2]] = io_m[...].astype(F32)
-    mid_x = slab_swap(mb, xm, ym, 3, 3)
-    start(mid_x)
-    mid_flags = x_flags(om, bm[0]) + y_flags(om, om_l, om_r, bm[0])
-    start(mid_flags)
     edge[0:2] = in_f[0:2].astype(F32)
     edge[2] = in_f[nz * xf - 1].astype(F32)
-
-    def row_prolong(own, extra, index, total, cols, col_own, col_extra, col_index):
-        shape = (own + extra, cols)
-        fine = logical(iota(shape, 0), own, extra) + own * index
-        coarse = logical(iota(shape, 1), col_own, col_extra) + col_own * col_index
-        return prolong_matrix(fine, coarse, total)
-
-    def lane_prolong(cells, rows):
-        shape = (rows, cells)
-        return prolong_matrix(iota(shape, 1), iota(shape, 0), cells)
-
-    def lane_bricks(cells, bricks, halves):
-        shape = (halves * LANES, cells)
-        brick = lax.div(iota(shape, 1), cells // (bricks * halves))
-        place = brick + lax.div(brick, bricks) * (LANES - bricks)
-        return (place == iota(shape, 0)).astype(BF16)
-
-    def screens(dest, occ_parts, own, extra_rows, bricks_y, lane_matrix, level):
-        count = dest.shape[0]
-        side = own // bricks_y
-        cols = ROWS * len(occ_parts)
-        shape = (dest.shape[1], cols)
-        brick = lax.div(logical(iota(shape, 0), own, extra_rows) + side, side) - 1
-        place = jnp.where(
-            brick < 0, ROWS + bricks_y - 1, jnp.where(brick >= bricks_y, 2 * ROWS, brick)
-        )
-        row_matrix = (place == iota(shape, 1)).astype(BF16)
-        for x in range(count):
-            flags = jnp.concatenate([part[x] for part in occ_parts], axis=0).astype(BF16)
-            wide = mm(flags, lane_matrix).astype(BF16)
-            dest[x] = weight[level] * (0.25 + mm(row_matrix, wide))
-
-    def along_y(v):
-        n = v.shape[0]
-        return pltpu.roll(v, 1, 0), pltpu.roll(v, n - 1, 0)
-
-    def z_up(v):
-        n = v.shape[1]
-        turned = pltpu.roll(v, 1, 1)
-        edge_lane = iota((v.shape[0], LANES), 1) == 0
-        fixed = jnp.where(edge_lane, 0.0, turned[:, 0:LANES])
-        return fixed if n == LANES else jnp.concatenate([fixed, turned[:, LANES:]], axis=1)
-
-    def z_down(v):
-        n = v.shape[1]
-        turned = pltpu.roll(v, n - 1, 1)
-        edge_lane = iota((v.shape[0], LANES), 1) == LANES - 1
-        fixed = jnp.where(edge_lane, 0.0, turned[:, n - LANES :])
-        return fixed if n == LANES else jnp.concatenate([turned[:, : n - LANES], fixed], axis=1)
-
-    loads["w"].wait()
-    lanes_c = lane_bricks(zc, bc[2], 1)
-    side_c = nz * xc // bc[0]
-    shape_c = (yc, zc)
-    row_c = iota(shape_c, 0)
-
-    def sum_c(v, twice):
-        yu, yd = along_y(v)
-        total = jnp.where(row_c < yc - 1, yd, 0.0) + z_down(v)
-        if twice:
-            total = total + jnp.where(row_c > 0, yu, 0.0) + z_up(v)
-        return total
-
-    def brick_of(own, side):
-        return lambda p: lax.div(own * iz + p + (side - PAD), side)
-
-    brick_c = brick_of(xc, side_c)
-
-    def coarse_w(p, carry):
-        r = cr[p]
-        place = xc * slab + p - PAD
-        keep = both(place >= 0, place < xc * slabs).astype(F32)
-        screen = cs[brick_c(p)]
-        cw[p] = keep * (screen * r - (cr[p - 1] + cr[p + 1] + sum_c(r, True)))
-        return carry
-
-    def coarse_moments(p, acc):
-        r, w = cr[p], cw[p]
-        image = cs[brick_c(p)] * w - 2.0 * (cw[p + 1] + sum_c(w, False))
-        return tuple(a + fold_rows(b) for a, b in zip(acc, (r * r, r * w, w * w, w * image)))
-
-    zero = jnp.zeros((ROWS, LANES), F32)
-    lane_index = iota((1, LANES), 1)
-
-    def spread_moments(acc, buf, send, recv, offsets, slot):
-        row = jnp.zeros((1, LANES), F32)
-        for k, a in enumerate(acc):
-            value = jnp.sum(jnp.sum(a, axis=0, keepdims=True), axis=1, keepdims=True)
-            row = jnp.where(lane_index == k, value, row)
-        buf[slot] = row
-        copies = []
-        for k, offset in enumerate(offsets):
-            c = pltpu.make_async_remote_copy(
-                src_ref=buf.at[slot], dst_ref=buf.at[slot], send_sem=send.at[k],
-                recv_sem=recv.at[k], device_id=at(offset), device_id_type=MESH,
-            )
-            c.start()
-            copies.append(c)
-        return copies
-
-    def solve(copies, buf):
-        for c in copies:
-            c.wait_recv()
-        total = [buf[k] for k in range(buf.shape[0])]
-        while len(total) > 1:
-            total = [sum(total[k : k + 2][1:], total[k]) for k in range(0, len(total), 2)]
-        return coefficients(*[
-            jnp.sum(jnp.where(lane_index == k, total[0], 0.0), axis=1, keepdims=True)
-            for k in range(4)
-        ])
-
-    flat_slot = (ix * ny + iy) * nz + iz
-    arrive(near)
-    screens(cs, [oc], yc, 0, bc[1], lanes_c, 0)
-    lax.fori_loop(PAD, PAD + xc + 1, coarse_w, 0, unroll=True)
-    acc = lax.fori_loop(PAD, PAD + xc, coarse_moments, (zero,) * 4, unroll=True)
-    coarse_copies = spread_moments(acc, ac, sc, rc, [o for o in peers if o[1] == 0], slab)
-
     pair_up, made_up = copy(
         edge.at[pl.ds(2, 1)], fb.at[pl.ds(PAD - 1, 1), 0:yf, own_z], above, iz, nz
     )
@@ -413,36 +389,91 @@
     fine_x += [(c, False, get_low) for c in made_up] + [(c, False, get_high) for c in made_dn]
     start(fine_x)
 
-    arrive(mid_x)
-    mid_y = y_swap(mb, xm, ym, 4, 3, 3, m_up, m_dn, m_fu, m_fd)
-    start(mid_y)
-    arrive(far)
-    lax.fori_loop(1, PAD, coarse_w, 0, unroll=True)
-    lax.fori_loop(PAD + xc + 1, PAD + xc + 3, coarse_w, 0, unroll=True)
-    mid_lanes = lane_prolong(zm, zc)
-    mid_rows = row_prolong(ym, ROWS, iy, ym * ny, yc, yc, 0, 0)
-    arrive(z_fine)
-    fine_flags = x_flags(of, bf[0]) + y_flags(of, of_l, of_r, bf[0])
-    start(fine_flags)
-    arrive(mid_flags)
-    lanes_m = lane_bricks(zm, bm[2], 1)
-    screens(ms, [om, om_l, om_r], ym, ROWS, bm[1], lanes_m, 1)
-
-    ka, kb = solve(coarse_copies, ac)
-    for j in range(xc + 6):
-        cx[j] = ka * cr[j + 1] + kb * cw[j + 1]
-    own_c = pl.ds(iz * xc, xc)
-    out_c[own_c] = cx[3 : 3 + xc]
-    outs = [(copy(out_c.at[own_c], out_c.at[own_c], partner), None, None)]
-    start(outs)
-
-    def prolong(src, tz, dst, lane_matrix, row_matrix):
-        n, rows, lanes = src.shape
-        high, low = split(src[...].reshape(n * rows, lanes))
+    def along_y(v):
+        n = v.shape[0]
+        return pltpu.roll(v, 1, 0), pltpu.roll(v, n - 1, 0)
+
+    def z_up(v):
+        n = v.shape[1]
+        turned = pltpu.roll(v, 1, 1)
+        edge_lane = iota((v.shape[0], LANES), 1) == 0
+        fixed = jnp.where(edge_lane, 0.0, turned[:, 0:LANES])
+        return fixed if n == LANES else jnp.concatenate([fixed, turned[:, LANES:]], axis=1)
+
+    def z_down(v):
+        n = v.shape[1]
+        turned = pltpu.roll(v, n - 1, 1)
+        edge_lane = iota((v.shape[0], LANES), 1) == LANES - 1
+        fixed = jnp.where(edge_lane, 0.0, turned[:, n - LANES :])
+        return fixed if n == LANES else jnp.concatenate([turned[:, : n - LANES], fixed], axis=1)
+
+    side_c = nz * xc // bc[0]
+    shape_c = (yc, zc)
+    row_c = iota(shape_c, 0)
+
+    def sum_c(v, twice):
+        yu, yd = along_y(v)
+        total = jnp.where(row_c < yc - 1, yd, 0.0) + z_down(v)
+        if twice:
+            total = total + jnp.where(row_c > 0, yu, 0.0) + z_up(v)
+        return total
+
+    def brick_of(own, side):
+        return lambda p: lax.div(own * iz + p + (side - PAD), side)
+
+    brick_c = brick_of(xc, side_c)
+
+    def coarse_w(p, carry):
+        r = cr[p]
+        place = xc * slab + p - PAD
+        keep = both(place >= 0, place < xc * slabs).astype(F32)
+        screen = cs[brick_c(p)]
+        cw[p] = keep * (screen * r - (cr[p - 1] + cr[p + 1] + sum_c(r, True)))
+        return carry
+
+    def coarse_moments(p, acc):
+        r, w = cr[p], cw[p]
+        image = cs[brick_c(p)] * w - 2.0 * (cw[p + 1] + sum_c(w, False))
+        return tuple(a + fold_rows(b) for a, b in zip(acc, (r * r, r * w, w * w, w * image)))
+
+    zero = jnp.zeros((ROWS, LANES), F32)
+    lane_index = iota((1, LANES), 1)
+
+    def spread_moments(values, buf, send, recv):
+        row = jnp.zeros((1, LANES), F32)
+        for k, a in values:
+            value = jnp.sum(jnp.sum(a, axis=0, keepdims=True), axis=1, keepdims=True)
+            row = jnp.where(lane_index == k, value, row)
+        slot = (ix * ny + iy) * nz + iz
+        buf[slot] = row
+        copies = []
+        for k, offset in enumerate(peers):
+            c = pltpu.make_async_remote_copy(
+                src_ref=buf.at[slot], dst_ref=buf.at[slot], send_sem=send.at[k],
+                recv_sem=recv.at[k], device_id=at(offset), device_id_type=MESH,
+            )
+            c.start()
+            copies.append(c)
+        return copies
+
+    def gathered(copies, buf):
+        for c in copies:
+            c.wait_recv()
+        total = [buf[k] for k in range(buf.shape[0])]
+        while len(total) > 1:
+            total = [sum(total[k : k + 2][1:], total[k]) for k in range(0, len(total), 2)]
+        return total[0]
+
+    def picked(row, test):
+        return jnp.sum(jnp.where(test, row, 0.0), axis=1, keepdims=True)
+
+    def prolong(values, tz, dst, lane_matrix, row_matrix):
+        n, rows, lanes = values.shape
+        high, low = split(values.reshape(n * rows, lanes))
         tz[...] = (mm(high, lane_matrix) + mm(low, lane_matrix)).reshape(tz.shape)
+        twice = jnp.concatenate([row_matrix, row_matrix], axis=1)
         for j in range(n):
-            high, low = split(tz[j])
-            dst[j] = mm(row_matrix, high) + mm(row_matrix, low)
+            dst[j] = mm(twice, jnp.concatenate(split(tz[j]), axis=0))
 
     def interpolate(t, g, own, begin, low, high):
         for p in range(PAD - low, PAD + own + high):
@@ -473,87 +504,180 @@
             for p in range(PAD + own, PAD + own + high):
                 ref[p] = empty
 
-    def run_depth(b, g, r, w, s, own, rows, index, total, side, r_low, r_high, unroll):
-        brick = brick_of(own, side)
-        shape = (ROWS, b.shape[2])
+    def row_mask(rows, index, total, lanes):
+        shape = (ROWS, lanes)
         row = logical(iota(shape, 0) + rows, rows, ROWS) + rows * index
-        mask = both(row >= 0, row < total).astype(F32)
-
-        def masked(v):
-            return jnp.concatenate([v[0:rows], v[rows:] * mask], axis=0)
-
-        def make_r(p, carry):
+        return both(row >= 0, row < total).astype(F32)
+
+    def masked(v, mask):
+        rows = v.shape[0] - ROWS
+        return jnp.concatenate([v[0:rows], v[rows:] * mask], axis=0)
+
+    def upward(ref, p, full, rows):
+        return ref[p + 1, 0:rows] + along_y(full)[1][0:rows] + z_down(full[0:rows])
+
+    arrive(near)
+    arrive(near_screens)
+    relay_wait(0)
+    relay_send(1)
+    lax.fori_loop(PAD, PAD + xc + 1, coarse_w, 0, unroll=True)
+    acc_c = lax.fori_loop(PAD, PAD + xc, coarse_moments, (zero,) * 4, unroll=True)
+    mid_lanes = lane_prolong(zm, zc)
+    mid_rows = row_prolong(ym, ROWS, iy, ym * ny, yc, yc, 0, 0)
+    arrive(far)
+    prolong(cr[1 : xc + 7], ctz, ct, mid_lanes, mid_rows)
+    interpolate(ct, g1, xm, -3, 4, 4)
+    lax.fori_loop(1, PAD, coarse_w, 0, unroll=True)
+    lax.fori_loop(PAD + xc + 1, PAD + xc + 3, coarse_w, 0, unroll=True)
+    prolong(cw[1 : xc + 7], ctz, ct, mid_lanes, mid_rows)
+    interpolate(ct, g2, xm, -3, 4, 4)
+    arrive(mid_flags)
+    screens(ms, 0, bm[0] + 2, [om, om_l, om_r], ym, ROWS, bm[1], lane_bricks(zm, bm[2], 1), 1)
+    mask_m = row_mask(ym, iy, ym * ny, zm)
+    brick_m = brick_of(xm, nz * xm // bm[0])
+
+    def mid_u(p, carry):
+        screen = 6.0 + ms[brick_m(p)]
+        for g, u in ((g1, u1), (g2, u2)):
             c = g[p]
-            value = b[p] - (6.0 + s[brick(p)]) * c
-            r[p] = masked(value + (g[p - 1] + g[p + 1]) + neighbours(c))
-            return carry
-
-        lax.fori_loop(PAD - r_low, PAD + own + r_high, make_r, 0, unroll=unroll)
-        clear(r, own, r_low, r_high)
-
-        def make_w(p, carry):
-            c = r[p]
-            w[p] = masked(s[brick(p)] * c - (r[p - 1] + r[p + 1]) - neighbours(c))
-            return carry
-
-        lax.fori_loop(PAD - r_low + 1, PAD + own + r_high - 1, make_w, 0, unroll=unroll)
-        clear(w, own, r_low - 1, r_high - 1)
-
-        def moments(p, acc):
-            rv, full = r[p, 0:rows], w[p]
-            wv = full[0:rows]
-            image = s[brick(p), 0:rows] * wv - 2.0 * (
-                w[p + 1, 0:rows] + along_y(full)[1][0:rows] + z_down(wv)
-            )
-            return tuple(
-                a + fold_rows(v) for a, v in zip(acc, (rv * rv, rv * wv, wv * wv, wv * image))
-            )
-
-        return lax.fori_loop(PAD, PAD + own, moments, (zero,) * 4, unroll=unroll)
-
-    prolong(cx, ctz, ct, mid_lanes, mid_rows)
-    interpolate(ct, mg, xm, -3, 4, 4)
+            u[p] = masked(screen * c - (g[p - 1] + g[p + 1]) - neighbours(c), mask_m)
+        return carry
+
+    lax.fori_loop(PAD - 3, PAD + xm + 3, mid_u, 0, unroll=True)
+    for ref in (u1, u2):
+        clear(ref, xm, 3, 3)
+    arrive(mid_x)
     arrive(mid_y)
-    y_merge(mb, ym, 4, m_fu, m_fd, 1)
-    acc = run_depth(mb, mg, mr, mw, ms, xm, ym, iy, ym * ny, nz * xm // bm[0], 3, 3, 2)
-    mid_copies = spread_moments(acc, am, sm, rm, peers, flat_slot)
-
+    y_merge(mb, ym, m_fu, m_fd, 1)
+    fields = ((mb, v0), (u1, v1), (u2, v2))
+
+    def mid_v(p, carry):
+        screen = ms[brick_m(p)]
+        for u, v in fields:
+            c = u[p]
+            v[p] = masked(screen * c - (u[p - 1] + u[p + 1]) - neighbours(c), mask_m)
+        return carry
+
+    lax.fori_loop(PAD - 2, PAD + xm + 2, mid_v, 0, unroll=True)
+    for ref in (v0, v1, v2):
+        clear(ref, xm, 2, 2)
+    pairs_m = ((0, 0), (1, 1), (2, 2), (0, 1), (0, 2), (1, 2))
+
+    def mid_moments(p, acc):
+        screen = ms[brick_m(p), 0:ym]
+        us = [u[p, 0:ym] for u, _ in fields]
+        full = [v[p] for _, v in fields]
+        vs = [v[0:ym] for v in full]
+        images = [
+            screen * v - 2.0 * upward(ref, p, f, ym) for v, f, (_, ref) in zip(vs, full, fields)
+        ]
+        values = [us[i] * us[j] for i, j in pairs_m] + [us[i] * vs[j] for i, j in pairs_m]
+        values += [vs[i] * vs[j] for i, j in pairs_m]
+        for i, j in pairs_m:
+            cross = vs[i] * images[j]
+            values.append(cross if i == j else 0.5 * (cross + vs[j] * images[i]))
+        return tuple(a + fold_rows(v) for a, v in zip(acc, values))
+
+    acc = lax.fori_loop(PAD, PAD + xm, mid_moments, (zero,) * 24, unroll=2)
+    relay_wait(1)
+    for k in range(2, rounds):
+        relay_send(k)
+        relay_wait(k)
+    slots = [(ROWS * (k // 6) + k % 6, a) for k, a in enumerate(acc)]
+    slots += [(4 * ROWS + k, a) for k, a in enumerate(acc_c)]
+    mid_copies = spread_moments(slots, am, sm, rm)
+
+    arrive(z_fine)
+    fine_flags = x_flags(of, bf[0]) + y_flags(of, of_l, of_r, bf[0])
+    start(fine_flags)
     arrive(fine_x)
-    fine_y = y_swap(fb, xf, yf, 2, 1, 2, f_up, f_dn, f_fu, f_fd)
+    fine_y = y_swap(fb, xf, yf, 1, 2, f_up, f_dn, f_fu, f_fd)
     start(fine_y)
     arrive(fine_flags)
     lanes_f = lane_bricks(zf, bf[2], nz)
-    screens(fs, [of, of_l, of_r], yf, ROWS, bf[1], lanes_f, 2)
+    screens(fs, 0, bf[0] + 2, [of, of_l, of_r], yf, ROWS, bf[1], lanes_f, 2)
     fine_lanes = lane_prolong(zf, zm)
     fine_rows = row_prolong(yf, ROWS, iy, yf * ny, ym + ROWS, ym, ROWS, iy)
     arrive(fine_y)
-    y_merge(fb, yf, 2, f_fu, f_fd, PAD - 1)
-    ka, kb = solve(mid_copies, am)
+    y_merge(fb, yf, f_fu, f_fd, PAD - 1)
+    total = gathered(mid_copies, am)
+    ka, kb = coefficients(*[picked(total, lane_index == 4 * ROWS + k) for k in range(4)])
+    weights = [None, ka * ka, kb * kb, -2.0 * ka, -2.0 * kb, 2.0 * ka * kb]
+    kind = lane_index % ROWS
+    scaled = total
+    for k in range(1, 6):
+        scaled = jnp.where(kind == k, total * weights[k], scaled)
+    place = lax.div(lane_index, ROWS)
+    km, kw = coefficients(*[
+        picked(scaled, both(place == k, kind < 6)) for k in range(4)
+    ])
+    parts = (
+        (g1, ka), (g2, kb), (mb, km), (u1, -km * ka), (u2, -km * kb),
+        (v0, kw), (v1, -kw * ka), (v2, -kw * kb),
+    )
     for p in range(2, xm + 6):
-        mx[p - 2] = mg[p] + ka * mr[p] + kb * mw[p]
-    own_m = pl.ds(iz * xm, xm)
-    out_m[own_m] = mx[2 : 2 + xm, 0:ym, :]
-    outs.append((copy(out_m.at[own_m], out_m.at[own_m], partner), None, None))
-    start(outs[1:])
-
-    prolong(mx, mtz, mt, fine_lanes, fine_rows)
+        value = parts[0][1] * parts[0][0][p]
+        for ref, factor in parts[1:]:
+            value = value + factor * ref[p]
+        mx[p - 2] = value
+    own_c, own_m = pl.ds(iz * xc, xc), pl.ds(iz * xm, xm)
+
+    prolong(mx[...], mtz, mt, fine_lanes, fine_rows)
     interpolate(mt, fg, xf, -2, 2, 3)
-    acc = run_depth(fb, fg, fr, fw, fs, xf, yf, iy, yf * ny, nz * xf // bf[0], 1, 2, 2)
-    fine_copies = spread_moments(acc, af, sf, rf, peers, flat_slot)
+    brick_f = brick_of(xf, nz * xf // bf[0])
+    mask_f = row_mask(yf, iy, yf * ny, zf)
+
+    def make_r(p, carry):
+        c = fg[p]
+        value = fb[p] - (6.0 + fs[brick_f(p)]) * c
+        fr[p] = masked(value + (fg[p - 1] + fg[p + 1]) + neighbours(c), mask_f)
+        return carry
+
+    lax.fori_loop(PAD - 1, PAD + xf + 2, make_r, 0, unroll=UNROLL)
+    clear(fr, xf, 1, 2)
+
+    def make_w(p, carry):
+        c = fr[p]
+        fw[p] = masked(fs[brick_f(p)] * c - (fr[p - 1] + fr[p + 1]) - neighbours(c), mask_f)
+        return carry
+
+    lax.fori_loop(PAD, PAD + xf + 1, make_w, 0, unroll=UNROLL)
+    clear(fw, xf, 0, 1)
+
+    def moments(p, acc):
+        rv, full = fr[p, 0:yf], fw[p]
+        wv = full[0:yf]
+        image = fs[brick_f(p), 0:yf] * wv - 2.0 * upward(fw, p, full, yf)
+        return tuple(
+            a + fold_rows(v) for a, v in zip(acc, (rv * rv, rv * wv, wv * wv, wv * image))
+        )
+
+    acc = lax.fori_loop(PAD, PAD + xf, moments, (zero,) * 4, unroll=UNROLL)
+    fine_copies = spread_moments(list(enumerate(acc)), af, sf, rf)
     their_z = pl.ds(pl.multiple_of(other * zh, LANES), zh)
     back = [
         (copy(src.at[PAD : PAD + xf, 0:yf, their_z], dst, partner), None, None)
         for src, dst in ((fg, tg), (fr, tr), (fw, tw))
     ]
     start(back)
-    for items in (near, far, z_fine, mid_x, mid_flags, fine_x, mid_y, fine_flags, fine_y, outs):
+    out_c[own_c] = ka * cr[PAD : PAD + xc] + kb * cw[PAD : PAD + xc]
+    out_m[own_m] = mx[2 : 2 + xm, 0:ym, :]
+    outs = [
+        (copy(out_c.at[own_c], out_c.at[own_c], partner), None, None),
+        (copy(out_m.at[own_m], out_m.at[own_m], partner), None, None),
+    ]
+    start(outs)
+    for items in (
+        near, near_screens, far, z_fine, mid_x, mid_flags, fine_x, mid_y, fine_flags, fine_y, outs
+    ):
         left(items)
-    for c in coarse_copies + mid_copies:
+    for c in mid_copies:
         c.wait_send()
     arrive(outs)
     arrive(back)
     left(back)
-    ka, kb = solve(fine_copies, af)
+    total = gathered(fine_copies, af)
+    ka, kb = coefficients(*[picked(total, lane_index == k) for k in range(4)])
     coef[0] = jnp.broadcast_to(ka, (ROWS, LANES))
     coef[1] = jnp.broadcast_to(kb, (ROWS, LANES))
     for c in fine_copies:
@@ -616,21 +740,25 @@
     scratch += [pltpu.SMEM(args[6].shape, F32), pltpu.SemaphoreType.DMA((7,))]
     scratch += [
         buf(xc + 8, yc, zc), buf(xc + 8, yc, zc), buf(occ_c.shape[0] + 2, yc, zc),
-        buf(xc + 6, yc, zc), buf(xc + 6, yc, zm), buf(xc + 6, *me),
+        buf(xc + 6, yc, zm), buf(xc + 6, *me),
         buf(occ_c.shape[0] + 2, ROWS, LANES),
-        buf(xm + 8, *me), buf(xm + 8, *me), buf(xm + 8, *me), buf(xm + 8, *me), buf(bm, *me),
+    ]
+    scratch += [buf(xm + 8, *me)] * 8
+    scratch += [
+        buf(bm, *me),
         buf(xm + 4, *me), buf(xm + 4, me[0], zf), buf(xm + 4, *fe),
         buf(bm, ROWS, LANES),
         buf(xm + 6, 4, zm), buf(xm + 6, 4, zm), buf(xm + 6, 4, zm), buf(xm + 6, 4, zm),
         buf(bm, ROWS, LANES), buf(bm, ROWS, LANES),
         buf(xf + 8, *fe), buf(bf, *fe), buf(bf, ROWS, nz * LANES),
         buf(xf + 2, yf, zh), buf(3, yf, zh),
-        buf(xf + 3, 2, zf), buf(xf + 3, 2, zf), buf(xf + 3, 2, zf), buf(xf + 3, 2, zf),
+        buf(xf + 3, 1, zf), buf(xf + 3, 2, zf), buf(xf + 3, 1, zf), buf(xf + 3, 2, zf),
         buf(bf, ROWS, nz * LANES), buf(bf, ROWS, nz * LANES),
-        buf(nx * nz, 1, LANES), buf(nx * ny * nz, 1, LANES), buf(nx * ny * nz, 1, LANES),
+        buf(nx * ny * nz, 1, LANES), buf(nx * ny * nz, 1, LANES),
     ]
-    for count in (48, nx * nz, nx * ny * nz, nx * ny * nz):
+    for count in (64, nx * ny * nz, nx * ny * nz):
         scratch += [pltpu.SemaphoreType.DMA((count,))] * 2
+    scratch += [pltpu.SemaphoreType.REGULAR((max(nx, ny),))]
     hbm = pl.BlockSpec(memory_space=pltpu.HBM)
     vmem = pl.BlockSpec(memory_space=pltpu.VMEM)
     field = pltpu.VMEM((xf + 8,) + fe, F32)

time: 34.5 us -> 31.6 us (0.916)
  Pallas kernels: 33.7 us -> 30.8 us
    pallas_call x1, Pallas kernels: 32.5 us -> 29.6 us  [shards(): pl.pallas_call(functools.partial(kernel, dims), out_shape=made_shapes, in...]
where the time goes in v2:
time: 31.6 us; the launch traced here: 31.5 us
  Pallas kernels  30.8 us (97%)
  between operations  0.64 us (2%)
    pallas_call x1, Pallas kernels, shards(): pl.pallas_call(functools.partial(kernel, dims), out_shape=made_shapes, in...  29.6 us
    pallas_call x1, Pallas kernels, shards(): pl.pallas_call(finish, out_shape=[jax.ShapeDtypeStruct(a.shape, F32) for...  1.2 us

profile of v2, /device:TPU:0, one launch (start us, length us, event | category | flops | bytes accessed | tf_op | source)
XLA Modules:
  0.0 31.5 jit_solution(16984100429809969339)
XLA Ops:
  0.6 29.6 %shard_map.94 = (f32[8,32,128]{2,1,0:T(8,128)S(1)}, f32[16,16,256]{2,1,0:T(8,128)S(1)}, f32[24,40,512]{2,1,0:T(8,128)S(1)}, f32[24,40,512]{2,1,0:T(8,128)S(1)}, ...) custom-call(bf16[8,32,128]{2,1,0:T(8,128)(2,1)} %rhs_c.1, ...), custom_call_target="tpu_custom_call" | custom-call | tf_op jit(solution)/shard_map/pallas_call | solution.py:769
  30.3 1.2 %shard_map.95 = (f32[8,32,128]{2,1,0:T(8,128)}, f32[16,16,256]{2,1,0:T(8,128)}, f32[32,32,256]{2,1,0:T(8,128)}) custom-call(f32[24,40,512]{2,1,0:T(8,128)S(1)} %get-tuple-element.12.g, f32[24,40,512]{2,1,0:T(8,128)S(1)} %get-tuple-element.13.r, f32[24,40,512]{2,1,0:T(8,128)S(1)} %get-tuple-element.14.w, f32[16,32,256]{2,1,0:T(8,128)S(1)} %get-tuple-element.15.tg, ...), custom_call_target="tpu_custom_call" | custom-call | tf_op jit(solution)/shard_map/pallas_call | solution.py:780

commit v3 on v2

v3 whole, which is shorter than its diff:
```python
import functools
import math

import jax
import jax.numpy as jnp
from jax import lax
from jax.experimental import pallas as pl
from jax.experimental.pallas import tpu as pltpu
from jax.sharding import PartitionSpec as P

MESH = pl.DeviceIdType.MESH
F32 = jnp.float32
BF16 = jnp.bfloat16
PAD = 4
ROWS = 8
TOP = 8
LANES = 128
VMEM_BYTES = 67043328
UNROLL = True


def iota(shape, dim):
    return lax.broadcasted_iota(jnp.int32, shape, dim)


def prolong_matrix(fine, coarse, total):
    base = lax.shift_right_arithmetic(fine, 1)
    beside = base + 2 * (fine & 1) - 1
    inside = jnp.logical_and(fine >= 0, fine < total)
    value = jnp.where(coarse == base, 0.75, jnp.where(coarse == beside, 0.25, 0.0))
    return jnp.where(inside, value, 0.0).astype(BF16)


def split(values):
    high = values.astype(BF16)
    return high, (values - high.astype(F32)).astype(BF16)


def mm(a, b):
    return jnp.dot(a, b, preferred_element_type=F32)


def fold_rows(values):
    total = values[0:ROWS]
    for row in range(ROWS, values.shape[0], ROWS):
        total = total + values[row : row + ROWS]
    out = total[:, 0:LANES]
    for lane in range(LANES, values.shape[1], LANES):
        out = out + total[:, lane : lane + LANES]
    return out


def coefficients(m0, n1, n2, n3):
    rho = n1 / m0
    spread = n2 - rho * n1
    bent = 6.0 * spread + (n3 - 2.0 * rho * n2 + rho * rho * n1)
    turn = jnp.where(bent > 0.0, jnp.maximum(spread, 0.0) / bent, 0.0)
    first = m0 / ((6.0 + rho) * m0 - jnp.maximum(spread, 0.0) * turn)
    second = -first * turn
    return first - second * rho, second


def kernel(
    dims,
    rhs_c, rhs_m, rhs_f, occ_c, occ_m, occ_f, weight_in,
    out_c, out_m, fg, fr, fw, tg, tr, tw, coef,
    in_c, in_m, in_f, io_c, io_m, io_f, weight, isem,
    cr, cw, cs, ctz, ct, oc,
    mb, g1, g2, u1, u2, v0, v1, v2, ms, mx, mtz, mt, om, m_up, m_dn, m_fu, m_fd, om_l, om_r,
    fb, fs, of, zsend, edge, f_up, f_dn, f_fu, f_fd, of_l, of_r,
    am, af, ss, rs, sm, rm, sf, rf, relay,
):
    nx, ny, nz = dims
    ix, iy, iz = lax.axis_index("gx"), lax.axis_index("gy"), lax.axis_index("gz")
    xc, yc, zc = rhs_c.shape
    xm, ym, zm = rhs_m.shape
    xf, yf, zh = rhs_f.shape
    zf = zh * nz
    xc, xm, xf = xc // nz, xm // nz, xf // nz
    cm, cf, ch = zm // LANES, zf // LANES, zh // LANES
    slab = ix * nz + iz
    slabs = nx * nz
    bc, bm, bf = occ_c.shape, occ_m.shape, occ_f.shape
    x_low, x_high = ix > 0, ix < nx - 1
    y_low, y_high = iy > 0, iy < ny - 1
    lower, upper = iz == 0, iz == 1
    first, last = slab == 0, slab == slabs - 1
    rows_c, rows_m, rows_f = (slice(TOP, TOP + n) for n in (yc, ym, yf))

    def both(a, b):
        return jnp.logical_and(a, b)

    def at(offset):
        return (
            lax.rem(ix + offset[0], nx), lax.rem(iy + offset[1], ny), lax.rem(iz + offset[2], nz)
        )

    loads = {}
    pairs = (
        ("c", rhs_c, in_c), ("oc", occ_c, io_c), ("om", occ_m, io_m), ("w", weight_in, weight),
        ("m", rhs_m, in_m), ("f", rhs_f, in_f), ("of", occ_f, io_f),
    )
    for k, (name, src, dst) in enumerate(pairs):
        loads[name] = pltpu.make_async_copy(src, dst, isem.at[k])
        loads[name].start()

    for ref in (oc, om, of):
        ref[...] = jnp.zeros_like(ref)

    barrier = pltpu.get_barrier_semaphore()
    peers = [(a, b, c) for a in range(nx) for b in range(ny) for c in range(nz)][1:]
    around = [(a, b) for a in (-1, 1, 0) for b in (-1, 1, 0)]

    def greet(semaphore, a, b, c):
        def send():
            pl.semaphore_signal(
                semaphore, inc=1, device_id=(ix + a, iy + b, c), device_id_type=MESH
            )

        tests = ((x_low, a < 0), (x_high, a > 0), (y_low, b < 0), (y_high, b > 0))
        there = [test for test, needed in tests if needed]
        if there:
            pl.when(functools.reduce(both, there))(send)
        else:
            send()

    for a, b in around:
        for c in range(1 if (a, b) == (0, 0) else 0, nz):
            greet(barrier, a, b, lax.rem(iz + c, nz))
    chips = (1 + jnp.where(x_low, 1, 0) + jnp.where(x_high, 1, 0)) * (
        1 + jnp.where(y_low, 1, 0) + jnp.where(y_high, 1, 0)
    )
    rounds = max(nx, ny) - 2

    def relay_send(k):
        if k < rounds:
            for a, b in around[:-1]:
                greet(relay.at[k], a, b, iz)

    def relay_wait(k):
        if k < rounds:
            pl.semaphore_wait(relay.at[k], chips - 1)

    def wipe(ref, planes):
        for p in planes:
            ref[p] = jnp.zeros(tuple(ref.shape[1:]), F32)

    @pl.when(first)
    def _():
        wipe(cr, range(0, 4))
        wipe(cs, (0,))
        wipe(mb, range(1, 4))
        wipe(fb, range(2, 4))
        for ref in (m_fu, m_fd):
            wipe(ref, range(0, 3))

    @pl.when(last)
    def _():
        wipe(cr, range(PAD + xc, PAD + xc + 4))
        wipe(cs, (bc[0] + 1,))
        wipe(mb, range(PAD + xm, PAD + xm + 3))
        wipe(fb, range(PAD + xf, PAD + xf + 2))
        for ref in (m_fu, m_fd):
            wipe(ref, range(xm + 3, xm + 6))

    @pl.when(jnp.logical_not(x_low))
    def _():
        for ref in (om_l, om_r, of_l, of_r):
            wipe(ref, (0,))

    @pl.when(jnp.logical_not(x_high))
    def _():
        for ref in (om_l, om_r, of_l, of_r):
            wipe(ref, (ref.shape[0] - 1,))

    @pl.when(jnp.logical_not(y_low))
    def _():
        for ref in (m_fu, f_fu, om_l, of_l):
            ref[...] = jnp.zeros_like(ref)

    @pl.when(jnp.logical_not(y_high))
    def _():
        for ref in (m_fd, f_fd, om_r, of_r):
            ref[...] = jnp.zeros_like(ref)

    loads["oc"].wait()
    oc[1 : 1 + bc[0], 0 : bc[1], 0 : bc[2]] = io_c[...].astype(F32)
    loads["om"].wait()
    om[1 : 1 + bm[0], 0 : bm[1], 0 : bm[2]] = io_m[...].astype(F32)
    loads["c"].wait()
    cr[pl.ds(PAD - 4 * iz, xc + 4), rows_c] = in_c[pl.ds(iz * (xc - 4), xc + 4)].astype(F32)

    pl.semaphore_wait(barrier, chips * nz - 1)
    relay_send(0)

    used = [0]

    def copy(src, dst, target, step=0, count=1):
        k = used[0]
        used[0] += count

        def made(j):
            return pltpu.make_async_remote_copy(
                src_ref=src, dst_ref=dst, send_sem=ss.at[k], recv_sem=rs.at[k + j],
                device_id=target, device_id_type=MESH,
            )

        return made(0) if count == 1 else (made(step), [made(j) for j in range(count)])

    def start(items):
        for c, can_send, _ in items:
            if can_send is None:
                c.start()
            elif can_send is not False:
                pl.when(can_send)(c.start)

    def arrive(items):
        for c, _, can_recv in items:
            if can_recv is None:
                c.wait_recv()
            elif can_recv is not False:
                pl.when(can_recv)(c.wait_recv)

    def left(items):
        for c, can_send, _ in items:
            if can_send is None:
                c.wait_send()
            elif can_send is not False:
                pl.when(can_send)(c.wait_send)

    above, below = {"gx": ix + 1, "gz": 0}, {"gx": ix - 1, "gz": 1}
    send_up, get_low = both(upper, x_high), both(lower, x_low)
    send_down, get_high = both(lower, x_low), both(upper, x_high)

    def slab_swap(view, own, width_low, width_high, skip_low=0, skip_high=0):
        stop, begin = PAD + own - skip_low, PAD + skip_high
        low = PAD - skip_low - width_low
        return [
            (copy(view(stop - width_low, width_low), view(low, width_low), above),
             send_up, get_low),
            (copy(view(begin, width_high), view(begin + own, width_high), below),
             send_down, get_high),
        ]

    def x_flags(occ, bricks):
        return [
            (copy(occ.at[bricks], occ.at[0], {"gx": ix + 1}), x_high, x_low),
            (copy(occ.at[1], occ.at[bricks + 1], {"gx": ix - 1}), x_low, x_high),
        ]

    def y_flags(occ, occ_l, occ_r, bricks):
        items = []
        flags = pl.ds(1, bricks)
        for dst, step, can_send, can_recv in (
            (occ_l, 1, y_high, y_low), (occ_r, -1, y_low, y_high)
        ):
            items.append((copy(occ.at[flags], dst.at[flags], {"gy": iy + step}), can_send, can_recv))
            items.append((copy(occ.at[bricks], dst.at[0], {"gx": ix + 1, "gy": iy + step}),
                          both(can_send, x_high), both(can_recv, x_low)))
            items.append((copy(occ.at[1], dst.at[bricks + 1], {"gx": ix - 1, "gy": iy + step}),
                          both(can_send, x_low), both(can_recv, x_high)))
        return items

    def row_prolong(own, margin, index, total, cols, col_first):
        shape = (own + ROWS, cols)
        fine = iota(shape, 0) - margin + own * index
        return prolong_matrix(fine, iota(shape, 1) + col_first, total)

    def lane_prolong(cells, rows):
        shape = (rows, cells)
        return prolong_matrix(iota(shape, 1), iota(shape, 0), cells)

    def lane_bricks(cells, bricks, halves):
        shape = (halves * LANES, cells)
        brick = lax.div(iota(shape, 1), cells // (bricks * halves))
        place = brick + lax.div(brick, bricks) * (LANES - bricks)
        return (place == iota(shape, 0)).astype(BF16)

    def screens(put, begin, count, occ_parts, own, margin, bricks_y, lane_matrix, level):
        side = own // bricks_y
        cols = ROWS * len(occ_parts)
        shape = (own + 2 * margin if margin == 0 else own + ROWS, cols)
        brick = lax.div(iota(shape, 0) - margin + side, side) - 1
        place = jnp.where(
            brick < 0, ROWS + bricks_y - 1, jnp.where(brick >= bricks_y, 2 * ROWS, brick)
        )
        row_matrix = (place == iota(shape, 1)).astype(BF16)
        flags = [part[begin + x] for x in range(count) for part in occ_parts]
        wide = mm(jnp.concatenate(flags, axis=0).astype(BF16), lane_matrix).astype(BF16)
        for x in range(count):
            cells = mm(row_matrix, wide[x * cols : (x + 1) * cols])
            put(begin + x, weight[level] * (0.25 + cells))

    def chunked(ref):
        def put(j, value):
            for c in range(ref.shape[1]):
                ref[j, c] = value[:, c * LANES : (c + 1) * LANES]

        return put

    def put_coarse(j, value):
        cs[j] = value

    def coarse_view(begin, count):
        return cr.at[pl.ds(begin, count), rows_c]

    def mid_view(begin, count):
        return mb.at[pl.ds(begin, count), :, rows_m]

    near = slab_swap(coarse_view, xc, 1, 2)
    start(near)
    mid_flags = x_flags(om, bm[0]) + y_flags(om, om_l, om_r, bm[0])
    start(mid_flags)
    loads["w"].wait()
    screens(put_coarse, 1, bc[0], [oc], yc, 0, bc[1], lane_bricks(zc, bc[2], 1), 0)
    near_screens = [
        (copy(cs.at[bc[0]], cs.at[0], above), send_up, get_low),
        (copy(cs.at[1], cs.at[bc[0] + 1], below), send_down, get_high),
    ]
    start(near_screens)
    far = slab_swap(coarse_view, xc, 3, 2, 1, 2)
    start(far)

    loads["m"].wait()
    held = pl.ds(3 - 3 * iz, xm + 3)
    for c in range(cm):
        cols = slice(c * LANES, (c + 1) * LANES)
        block = in_m[pl.ds(iz * (xm - 3), xm + 3), :, cols].astype(F32)
        mb[pl.ds(PAD - 3 * iz, xm + 3), c, rows_m] = block
        m_up[held, c] = block[:, ym - 4 : ym]
        m_dn[held, c] = block[:, 0:4]
    mid_x = slab_swap(mid_view, xm, 3, 3)
    start(mid_x)
    mid_y = []
    for src, dst, step, can_send, can_recv in (
        (m_up, m_fu, 1, y_high, y_low), (m_dn, m_fd, -1, y_low, y_high)
    ):
        side = {"gy": iy + step}
        mid_y.append((copy(src.at[held], dst.at[held], side), can_send, can_recv))
        mid_y.append((copy(src.at[xm : xm + 3], dst.at[0:3], {**above, **side}),
                      both(can_send, send_up), both(can_recv, get_low)))
        mid_y.append((copy(src.at[3:6], dst.at[xm + 3 : xm + 6], {**below, **side}),
                      both(can_send, send_down), both(can_recv, get_high)))
    start(mid_y)

    loads["f"].wait()
    other = 1 - iz
    own_z, their_z = pl.ds(iz * ch, ch), pl.ds(other * ch, ch)

    def half_plane(p, c):
        return in_f[p, :, c * LANES : (c + 1) * LANES].astype(F32)

    def fill_fine(j, carry):
        for c in range(ch):
            zsend[j, c] = half_plane(other * (xf - 2) + j, c)
            fb[PAD - 2 * iz + j, iz * ch + c, rows_f] = half_plane(iz * (xf - 2) + j, c)
        return carry

    lax.fori_loop(0, xf + 2, fill_fine, 0, unroll=2)
    loads["of"].wait()
    own_flags = pl.ds(pl.multiple_of(iz * LANES, LANES), LANES)
    flags = jnp.concatenate(
        [io_f[...].astype(F32), jnp.zeros((bf[0], bf[1], LANES - bf[2]), F32)], axis=2
    )
    of[1 : 1 + bf[0], 0 : bf[1], own_flags] = flags
    partner = {"gz": other}
    z_fine = [
        (copy(zsend, fb.at[pl.ds(PAD - 2 * other, xf + 2), own_z, rows_f], partner), None, None),
        (copy(of.at[pl.ds(1, bf[0]), :, own_flags], of.at[pl.ds(1, bf[0]), :, own_flags], partner),
         None, None),
    ]
    start(z_fine[::-1])
    for c in range(ch):
        for k, p in enumerate((0, 1, nz * xf - 1)):
            edge[k, c] = half_plane(p, c)
    pair_up, made_up = copy(
        edge.at[pl.ds(2, 1)], fb.at[pl.ds(PAD - 1, 1), own_z, rows_f], above, iz, nz
    )
    pair_dn, made_dn = copy(
        edge.at[pl.ds(0, 2)], fb.at[pl.ds(PAD + xf, 2), own_z, rows_f], below, iz, nz
    )
    fine_x = [(pair_up, x_high, False), (pair_dn, x_low, False)]
    fine_x += [(c, False, get_low) for c in made_up] + [(c, False, get_high) for c in made_dn]
    start(fine_x)

    def wipe_rims(ref, own):
        shape = tuple(ref.shape)
        empty = jnp.zeros(shape[1:-2] + (TOP, LANES), F32)

        def one(p, carry):
            if len(shape) == 3:
                ref[p, 0:TOP] = empty
                ref[p, TOP + own :] = empty
            else:
                ref[p, :, 0:TOP] = empty
                ref[p, :, TOP + own :] = empty
            return carry

        lax.fori_loop(0, shape[0], one, 0)

    for ref in (cr, cw):
        wipe_rims(ref, yc)
    for ref in (mb, g1, g2, u1, u2, v0, v1, v2):
        wipe_rims(ref, ym)

    def z_lower(chunks):
        turned = [pltpu.roll(v, 1, 1) for v in chunks]
        edge_lane = iota(chunks[0].shape, 1) == 0
        return [
            jnp.where(edge_lane, turned[c - 1] if c else 0.0, turned[c])
            for c in range(len(chunks))
        ]

    def z_upper(chunks):
        turned = [pltpu.roll(v, LANES - 1, 1) for v in chunks]
        edge_lane = iota(chunks[0].shape, 1) == LANES - 1
        return [
            jnp.where(edge_lane, turned[c + 1] if c + 1 < len(chunks) else 0.0, turned[c])
            for c in range(len(chunks))
        ]

    def neighbours(load, chunks):
        low, high = z_lower(chunks), z_upper(chunks)
        return [
            (load(c, -1, 0) + load(c, 1, 0)) + (load(c, 0, -1) + load(c, 0, 1)) + (low[c] + high[c])
            for c in range(len(chunks))
        ]

    def later(load, chunks):
        high = z_upper(chunks)
        return [load(c, 1, 0) + load(c, 0, 1) + high[c] for c in range(len(chunks))]

    def view_of(ref, p, begin, count):
        def load(c, dx, dy):
            if len(ref.shape) == 3:
                return ref[p + dx, begin + dy : begin + dy + count]
            return ref[p + dx, c, begin + dy : begin + dy + count]

        return load, [load(c, 0, 0) for c in range(1 if len(ref.shape) == 3 else ref.shape[1])]

    def brick_of(own, side):
        return lambda p: lax.div(own * iz + p + (side - PAD), side)

    brick_c = brick_of(xc, nz * xc // bc[0])

    def coarse_w(p, carry):
        load, chunks = view_of(cr, p, TOP, yc)
        place = xc * slab + p - PAD
        keep = both(place >= 0, place < xc * slabs).astype(F32)
        cw[p, rows_c] = keep * (cs[brick_c(p)] * chunks[0] - neighbours(load, chunks)[0])
        return carry

    def coarse_moments(p, acc):
        load, chunks = view_of(cw, p, TOP, yc)
        r, w = cr[p, rows_c], chunks[0]
        image = cs[brick_c(p)] * w - 2.0 * later(load, chunks)[0]
        return tuple(a + fold_rows(b) for a, b in zip(acc, (r * r, r * w, w * w, w * image)))

    zero = jnp.zeros((ROWS, LANES), F32)
    lane_index = iota((1, LANES), 1)

    def spread_moments(values, buf, send, recv):
        row = jnp.zeros((1, LANES), F32)
        for k, a in values:
            value = jnp.sum(jnp.sum(a, axis=0, keepdims=True), axis=1, keepdims=True)
            row = jnp.where(lane_index == k, value, row)
        slot = (ix * ny + iy) * nz + iz
        buf[slot] = row
        copies = []
        for k, offset in enumerate(peers):
            c = pltpu.make_async_remote_copy(
                src_ref=buf.at[slot], dst_ref=buf.at[slot], send_sem=send.at[k],
                recv_sem=recv.at[k], device_id=at(offset), device_id_type=MESH,
            )
            c.start()
            copies.append(c)
        return copies

    def gathered(copies, buf):
        for c in copies:
            c.wait_recv()
        total = [buf[k] for k in range(buf.shape[0])]
        while len(total) > 1:
            total = [sum(total[k : k + 2][1:], total[k]) for k in range(0, len(total), 2)]
        return total[0]

    def picked(row, test):
        return jnp.sum(jnp.where(test, row, 0.0), axis=1, keepdims=True)

    def prolong(values, tz, put, lane_matrix, row_matrix):
        n, rows, lanes = values.shape
        high, low = split(values.reshape(n * rows, lanes))
        tz[...] = (mm(high, lane_matrix) + mm(low, lane_matrix)).reshape(tz.shape)
        twice = jnp.concatenate([row_matrix, row_matrix], axis=1)
        for j in range(n):
            put(j, mm(twice, jnp.concatenate(split(tz[j]), axis=0)))

    def interpolate(t, offset, count, g, own, begin, low, high, top):
        rows = t.shape[2]
        for p in range(PAD - low, PAD + own + high):
            m = p - PAD
            j = m // 2
            beside = min(max(j + (1 if m % 2 else -1) - begin, 0), count - 1)
            near_weight, side_weight = 0.75, 0.25
            if not 0 <= m < own:
                place = own * slab + m
                keep = both(place >= 0, place < own * slabs).astype(F32)
                near_weight, side_weight = 0.75 * keep, 0.25 * keep
            for c in range(t.shape[1]):
                g[p, c, top : top + rows] = (
                    near_weight * t[offset + j - begin, c] + side_weight * t[offset + beside, c]
                )

    def clear(ref, own, low, high):
        @pl.when(first)
        def _():
            wipe(ref, range(PAD - low, PAD))

        @pl.when(last)
        def _():
            wipe(ref, range(PAD + own, PAD + own + high))

    def row_masks(rows, margin, index, total):
        row = iota((rows + ROWS, LANES), 0) - margin + rows * index
        mask = both(row >= 0, row < total).astype(F32)
        return mask[0:ROWS], mask[rows:]

    def masked(v, masks):
        rows = v.shape[0] - ROWS
        return jnp.concatenate([v[0:ROWS] * masks[0], v[ROWS:rows], v[rows:] * masks[1]], axis=0)

    arrive(near)
    arrive(near_screens)
    relay_wait(0)
    relay_send(1)
    lax.fori_loop(PAD, PAD + xc + 1, coarse_w, 0, unroll=True)
    acc_c = lax.fori_loop(PAD, PAD + xc, coarse_moments, (zero,) * 4, unroll=True)
    mid_top = TOP - 4
    mid_lanes = lane_prolong(zm, zc)
    mid_rows = row_prolong(ym, 4, iy, ym * ny, yc, 0)
    arrive(mid_flags)
    screens(
        chunked(ms), 0, bm[0] + 2, [om, om_l, om_r], ym, 4, bm[1], lane_bricks(zm, bm[2], 1), 1
    )
    arrive(z_fine)
    fine_flags = x_flags(of, bf[0]) + y_flags(of, of_l, of_r, bf[0])
    start(fine_flags)
    arrive(far)
    lax.fori_loop(1, PAD, coarse_w, 0, unroll=True)
    lax.fori_loop(PAD + xc + 1, PAD + xc + 3, coarse_w, 0, unroll=True)
    count_c = xc + 6
    prolong(
        jnp.concatenate([cr[1 : 1 + count_c, rows_c], cw[1 : 1 + count_c, rows_c]], axis=0),
        ctz, chunked(ct), mid_lanes, mid_rows,
    )
    for k, ref in enumerate((g1, g2)):
        interpolate(ct, k * count_c, count_c, ref, xm, -3, 4, 4, mid_top)
    masks_m = row_masks(ym, 4, iy, ym * ny)
    brick_m = brick_of(xm, nz * xm // bm[0])
    window_m = slice(mid_top, mid_top + ym + ROWS)

    def mid_u(p, carry):
        brick = brick_m(p)
        for g, u in ((g1, u1), (g2, u2)):
            load, chunks = view_of(g, p, mid_top, ym + ROWS)
            for c, beside in enumerate(neighbours(load, chunks)):
                u[p, c, window_m] = masked((6.0 + ms[brick, c]) * chunks[c] - beside, masks_m)
        return carry

    lax.fori_loop(PAD - 3, PAD + xm + 3, mid_u, 0, unroll=True)
    for ref in (u1, u2):
        clear(ref, xm, 3, 3)
    arrive(mid_x)
    arrive(mid_y)
    for c in range(cm):
        mb[1 : xm + 7, c, TOP - 4 : TOP] = m_fu[:, c]
        mb[1 : xm + 7, c, TOP + ym : TOP + ym + 4] = m_fd[:, c]
    fields = ((mb, v0), (u1, v1), (u2, v2))

    def mid_v(p, carry):
        brick = brick_m(p)
        for u, v in fields:
            load, chunks = view_of(u, p, mid_top, ym + ROWS)
            for c, beside in enumerate(neighbours(load, chunks)):
                v[p, c, window_m] = masked(ms[brick, c] * chunks[c] - beside, masks_m)
        return carry

    lax.fori_loop(PAD - 2, PAD + xm + 2, mid_v, 0, unroll=True)
    for ref in (v0, v1, v2):
        clear(ref, xm, 2, 2)
    pairs_m = ((0, 0), (1, 1), (2, 2), (0, 1), (0, 2), (1, 2))

    def mid_moments(p, acc):
        brick = brick_m(p)
        views = [view_of(v, p, TOP, ym) for _, v in fields]
        beside = [later(load, chunks) for load, chunks in views]
        for c in range(cm):
            screen = ms[brick, c, 4 : 4 + ym]
            us = [u[p, c, rows_m] for u, _ in fields]
            vs = [chunks[c] for _, chunks in views]
            images = [screen * v - 2.0 * b[c] for v, b in zip(vs, beside)]
            values = [us[i] * us[j] for i, j in pairs_m] + [us[i] * vs[j] for i, j in pairs_m]
            values += [vs[i] * vs[j] for i, j in pairs_m]
            for i, j in pairs_m:
                cross = vs[i] * images[j]
                values.append(cross if i == j else 0.5 * (cross + vs[j] * images[i]))
            acc = tuple(a + fold_rows(v) for a, v in zip(acc, values))
        return acc

    acc = lax.fori_loop(PAD, PAD + xm, mid_moments, (zero,) * 24, unroll=2)
    relay_wait(1)
    for k in range(2, rounds):
        relay_send(k)
        relay_wait(k)
    slots = [(ROWS * (k // 6) + k % 6, a) for k, a in enumerate(acc)]
    slots += [(4 * ROWS + k, a) for k, a in enumerate(acc_c)]
    mid_copies = spread_moments(slots, am, sm, rm)

    arrive(fine_x)
    span = slice(PAD - 1, PAD + xf + 2)
    for c in range(cf):
        f_up[:, c] = fb[span, c, TOP + yf - 1 : TOP + yf]
        f_dn[:, c] = fb[span, c, TOP : TOP + 2]
    fine_y = [
        (copy(f_up, f_fu, {"gy": iy + 1}), y_high, y_low),
        (copy(f_dn, f_fd, {"gy": iy - 1}), y_low, y_high),
    ]
    start(fine_y)
    for ref in (fg, fr, fw):
        wipe_rims(ref, yf)
    fine_lanes = lane_prolong(zf, zm)
    fine_rows = row_prolong(yf, 2, iy, yf * ny, ym + ROWS, ym * iy - 4)
    masks_f = row_masks(yf, 2, iy, yf * ny)
    arrive(fine_flags)
    screens(
        chunked(fs), 0, bf[0] + 2, [of, of_l, of_r], yf, 2, bf[1], lane_bricks(zf, bf[2], nz), 2
    )
    arrive(fine_y)
    for c in range(cf):
        fb[span, c, TOP - 1 : TOP] = f_fu[:, c]
        fb[span, c, TOP + yf : TOP + yf + 2] = f_fd[:, c]
    total = gathered(mid_copies, am)
    ka, kb = coefficients(*[picked(total, lane_index == 4 * ROWS + k) for k in range(4)])
    weights = [None, ka * ka, kb * kb, -2.0 * ka, -2.0 * kb, 2.0 * ka * kb]
    kind = lane_index % ROWS
    scaled = total
    for k in range(1, 6):
        scaled = jnp.where(kind == k, total * weights[k], scaled)
    place = lax.div(lane_index, ROWS)
    km, kw = coefficients(*[
        picked(scaled, both(place == k, kind < 6)) for k in range(4)
    ])
    parts = (
        (g1, ka), (g2, kb), (mb, km), (u1, -km * ka), (u2, -km * kb),
        (v0, kw), (v1, -kw * ka), (v2, -kw * kb),
    )
    for p in range(2, xm + 6):
        for c in range(cm):
            value = parts[0][1] * parts[0][0][p, c, window_m]
            for ref, factor in parts[1:]:
                value = value + factor * ref[p, c, window_m]
            mx[p - 2, :, c * LANES : (c + 1) * LANES] = value
    own_c, own_m = pl.ds(iz * xc, xc), pl.ds(iz * xm, xm)

    prolong(mx[...], mtz, chunked(mt), fine_lanes, fine_rows)
    fine_top = TOP - 2
    interpolate(mt, 0, mt.shape[0], fg, xf, -2, 2, 3, fine_top)
    brick_f = brick_of(xf, nz * xf // bf[0])
    window_f = slice(fine_top, fine_top + yf + ROWS)

    def make_r(p, carry):
        brick = brick_f(p)
        load, chunks = view_of(fg, p, fine_top, yf + ROWS)
        for c, beside in enumerate(neighbours(load, chunks)):
            value = fb[p, c, window_f] - (6.0 + fs[brick, c]) * chunks[c] + beside
            fr[p, c, window_f] = masked(value, masks_f)
        return carry

    lax.fori_loop(PAD - 1, PAD + xf + 2, make_r, 0, unroll=UNROLL)
    clear(fr, xf, 1, 2)

    def make_w(p, carry):
        brick = brick_f(p)
        load, chunks = view_of(fr, p, fine_top, yf + ROWS)
        for c, beside in enumerate(neighbours(load, chunks)):
            fw[p, c, window_f] = masked(fs[brick, c] * chunks[c] - beside, masks_f)
        return carry

    lax.fori_loop(PAD, PAD + xf + 1, make_w, 0, unroll=UNROLL)
    clear(fw, xf, 0, 1)

    def moments(p, acc):
        brick = brick_f(p)
        load, chunks = view_of(fw, p, TOP, yf)
        for c, beside in enumerate(later(load, chunks)):
            r, w = fr[p, c, rows_f], chunks[c]
            image = fs[brick, c, 2 : 2 + yf] * w - 2.0 * beside
            acc = tuple(a + fold_rows(v) for a, v in zip(acc, (r * r, r * w, w * w, w * image)))
        return acc

    acc = lax.fori_loop(PAD, PAD + xf, moments, (zero,) * 4, unroll=UNROLL)
    fine_copies = spread_moments(list(enumerate(acc)), af, sf, rf)
    back = [
        (copy(src.at[PAD : PAD + xf, their_z, rows_f], dst, partner), None, None)
        for src, dst in ((fg, tg), (fr, tr), (fw, tw))
    ]
    start(back)
    out_c[own_c] = ka * cr[PAD : PAD + xc, rows_c] + kb * cw[PAD : PAD + xc, rows_c]
    out_m[own_m] = mx[2 : 2 + xm, 4 : 4 + ym, :]
    outs = [
        (copy(out_c.at[own_c], out_c.at[own_c], partner), None, None),
        (copy(out_m.at[own_m], out_m.at[own_m], partner), None, None),
    ]
    start(outs)
    for items in (
        near, near_screens, far, z_fine, mid_x, mid_flags, fine_x, mid_y, fine_flags, fine_y, outs
    ):
        left(items)
    for c in mid_copies:
        c.wait_send()
    arrive(outs)
    arrive(back)
    left(back)
    total = gathered(fine_copies, af)
    ka, kb = coefficients(*[picked(total, lane_index == k) for k in range(4)])
    coef[0] = jnp.broadcast_to(ka, (ROWS, LANES))
    coef[1] = jnp.broadcast_to(kb, (ROWS, LANES))
    for c in fine_copies:
        c.wait_send()


def finish(g, r, w, tg, tr, tw, coef, sol_c, sol_m, out_c, out_m, out_f, buf, sem):
    iz = lax.axis_index("gz")
    xs, ch, yf, _ = tg.shape
    small = [
        pltpu.make_async_copy(sol_c, out_c, sem.at[0]),
        pltpu.make_async_copy(sol_m, out_m, sem.at[1]),
    ]
    for c in small:
        c.start()
    ka, kb = coef[0, 0:1, 0:1], coef[1, 0:1, 0:1]
    rows = slice(TOP, TOP + yf)
    parts = 2
    step = xs // parts
    copies = list(small)
    for part in range(parts):
        for side in range(2):
            place = (iz if side == 0 else 1 - iz) * xs

            def one(x, carry):
                for c in range(ch):
                    if side == 0:
                        p, k = x + PAD, iz * ch + c
                        value = g[p, k, rows] + ka * r[p, k, rows] + kb * w[p, k, rows]
                    else:
                        value = tg[x, c] + ka * tr[x, c] + kb * tw[x, c]
                    buf[place + x, :, c * LANES : (c + 1) * LANES] = value
                return carry

            lax.fori_loop(part * step, part * step + step, one, 0, unroll=2)
            span = pl.ds(place + part * step, step)
            c = pltpu.make_async_copy(buf.at[span], out_f.at[span], sem.at[2 + 2 * part + side])
            c.start()
            copies.append(c)
    for c in copies:
        c.wait()


def shards(dims, *args):
    nx, ny, nz = dims
    rhs_c, rhs_m, rhs_f, occ_c, occ_m, occ_f, _ = args
    xc, yc, zc = rhs_c.shape
    xm, ym, zm = rhs_m.shape
    xf, yf, zh = rhs_f.shape
    zf = zh * nz
    xc, xm, xf = xc // nz, xm // nz, xf // nz
    cm, cf, ch = zm // LANES, zf // LANES, zh // LANES

    def buf(*shape):
        return pltpu.VMEM(shape, F32)

    def row(count, chunks, rows):
        return buf(count, chunks, rows, LANES)

    bm, bf = occ_m.shape[0] + 2, occ_f.shape[0] + 2
    scratch = [
        pltpu.VMEM(a.shape, a.dtype) for a in (rhs_c, rhs_m, rhs_f, occ_c, occ_m, occ_f)
    ]
    scratch += [pltpu.SMEM(args[6].shape, F32), pltpu.SemaphoreType.DMA((7,))]
    scratch += [
        buf(xc + 8, yc + 2 * TOP, zc), buf(xc + 8, yc + 2 * TOP, zc),
        buf(occ_c.shape[0] + 2, yc, zc),
        buf(2 * (xc + 6), yc, zm), row(2 * (xc + 6), cm, ym + ROWS),
        buf(occ_c.shape[0] + 2, ROWS, LANES),
    ]
    scratch += [row(xm + 8, cm, ym + 2 * TOP)] * 8
    scratch += [
        row(bm, cm, ym + ROWS),
        buf(xm + 4, ym + ROWS, zm), buf(xm + 4, ym + ROWS, zf), row(xm + 4, cf, yf + ROWS),
        buf(bm, ROWS, LANES),
        row(xm + 6, cm, 4), row(xm + 6, cm, 4), row(xm + 6, cm, 4), row(xm + 6, cm, 4),
        buf(bm, ROWS, LANES), buf(bm, ROWS, LANES),
        row(xf + 8, cf, yf + 2 * TOP), row(bf, cf, yf + ROWS), buf(bf, ROWS, nz * LANES),
        row(xf + 2, ch, yf), row(3, ch, yf),
        row(xf + 3, cf, 1), row(xf + 3, cf, 2), row(xf + 3, cf, 1), row(xf + 3, cf, 2),
        buf(bf, ROWS, nz * LANES), buf(bf, ROWS, nz * LANES),
        buf(nx * ny * nz, 1, LANES), buf(nx * ny * nz, 1, LANES),
    ]
    for count in (64, nx * ny * nz, nx * ny * nz):
        scratch += [pltpu.SemaphoreType.DMA((count,))] * 2
    scratch += [pltpu.SemaphoreType.REGULAR((max(nx, ny),))]
    hbm = pl.BlockSpec(memory_space=pltpu.HBM)
    vmem = pl.BlockSpec(memory_space=pltpu.VMEM)
    field = pltpu.VMEM((xf + 8, cf, yf + 2 * TOP, LANES), F32)
    half = pltpu.VMEM((xf, ch, yf, LANES), F32)
    made_shapes = [pltpu.VMEM(a.shape, F32) for a in args[:2]]
    made_shapes += [field] * 3 + [half] * 3 + [pltpu.VMEM((2, ROWS, LANES), F32)]
    room = sum(4 * math.prod(a.shape) for a in made_shapes)
    made = pl.pallas_call(
        functools.partial(kernel, dims),
        out_shape=made_shapes,
        in_specs=[hbm] * 7,
        out_specs=[vmem] * 9,
        scratch_shapes=scratch,
        compiler_params=pltpu.CompilerParams(
            collective_id=0, has_side_effects=True, vmem_limit_bytes=VMEM_BYTES - room
        ),
    )(*args)
    sol_c, sol_m, fields = made[0], made[1], made[2:]
    return pl.pallas_call(
        finish,
        out_shape=[jax.ShapeDtypeStruct(a.shape, F32) for a in args[:3]],
        in_specs=[vmem] * 9,
        out_specs=[hbm] * 3,
        scratch_shapes=[pltpu.VMEM(rhs_f.shape, F32), pltpu.SemaphoreType.DMA((6,))],
        compiler_params=pltpu.CompilerParams(vmem_limit_bytes=16 * 1024 * 1024),
    )(*fields, sol_c, sol_m)


def solution(mesh):
    dims = tuple(mesh.shape[axis] for axis in ("gx", "gy", "gz"))
    in_specs = (
        P("gx", None, None), P("gx", "gy", None), P("gx", "gy", "gz"),
        P("gx", None, None), P("gx", "gy", None), P("gx", "gy", "gz"), P(),
    )
    out_specs = (P("gx", None, None), P("gx", "gy", None), P("gx", "gy", "gz"))
    return jax.shard_map(
        functools.partial(shards, dims), mesh=mesh, in_specs=in_specs, out_specs=out_specs,
        check_vma=False,
    )
```

time: 31.6 us -> 28.5 us (0.902)
  Pallas kernels: 30.8 us -> 27.8 us
    pallas_call x1, Pallas kernels: 29.6 us -> 26.6 us  [shards(): pl.pallas_call(functools.partial(kernel, dims), out_shape=made_shapes, in...]
where the time goes in v3:
time: 28.5 us; the launch traced here: 28.4 us
  Pallas kernels  27.8 us (98%)
  between operations  0.64 us (2%)
    pallas_call x1, Pallas kernels, shards(): pl.pallas_call(functools.partial(kernel, dims), out_shape=made_shapes, in...  26.6 us
    pallas_call x1, Pallas kernels, shards(): pl.pallas_call(finish, out_shape=[jax.ShapeDtypeStruct(a.shape, F32) for...  1.2 us

profile of v3, /device:TPU:0, one launch (start us, length us, event | category | flops | bytes accessed | tf_op | source)
XLA Modules:
  0.0 28.4 jit_solution(10981186386005417414)
XLA Ops:
  0.6 26.6 %shard_map.94 = (f32[8,32,128]{2,1,0:T(8,128)S(1)}, f32[16,16,256]{2,1,0:T(8,128)S(1)}, f32[24,4,48,128]{3,2,1,0:T(8,128)S(1)}, f32[24,4,48,128]{3,2,1,0:T(8,128...) custom-call(bf16[8,32,128]{2,1,0:T(8,128)(2,1)} %rhs_c.1, ...), custom_call_target="tpu_custom_call" | custom-call | tf_op jit(solution)/shard_map/pallas_call | solution.py:819
  27.2 1.2 %shard_map.95 = (f32[8,32,128]{2,1,0:T(8,128)}, f32[16,16,256]{2,1,0:T(8,128)}, f32[32,32,256]{2,1,0:T(8,128)}) custom-call(f32[24,4,48,128]{3,2,1,0:T(8,128)S(1)} %get-tuple-element.12.g, f32[24,4,48,128]{3,2,1,0:T(8,128)S(1)} %get-tuple-element.13.r, f32[24,4,48,128]{3,2,1,0:T(8,128)S(1)} %get-tuple-element.14.w, ...), custom_call_target="tpu_custom_call" | custom-call | tf_op jit(solution)/shard_map/pallas_call | solution.py:830
